TPU v7x, 16 devices: a 4x2x1 block of a 4x4x8 slice. The times are simulated.
16 devices in a mesh: dp: 2 (over y, z), sp: 8 (over x, core).
Axes of the slice: x: 4, y: 2, z: 1, core: 2. Of those that a mesh axis runs over, the one named last changes fastest.
The devices are a block of a 4x4x8 slice.
Arguments:
- hidden: bfloat16 [4096, 6144], P(('dp', 'sp')), parts along dimension 0
- w_q: bfloat16 [6144, 6144], replicated
- w_k: bfloat16 [6144, 1024], replicated
- w_v: bfloat16 [6144, 1024], replicated
- w_o: bfloat16 [6144, 6144], replicated
- expert_ids: int32 [4096, 2], P(('dp', 'sp')), parts along dimension 0
- router_probs: float32 [4096, 8], P(('dp', 'sp')), parts along dimension 0
Outputs:
- output 1: bfloat16 [4096, 6144], P(('dp', 'sp')), parts along dimension 0
- output 2: bfloat16 [16, 2048, 6144], P(('dp', 'sp')), parts along dimension 0
There are 2 independent parts. A program takes and returns all parts, laid end to end along the dimension named above; an argument that names none is the same for every part.
All inputs are finite; a program needn't handle non-finite values.
Results may differ from a plain program's by a relative error of at most 0.00967614.
Values are sent between devices in bfloat16 or wider.
A program may use at most 768 MiB of HBM per device.

v0:
```python
import math
import jax
import jax.numpy as jnp
from jax import lax
from jax.sharding import PartitionSpec as P

HEAD_DIM = 128
SCORE_SCALE = 1.0 / math.sqrt(HEAD_DIM)


def route_rows(hidden_out, expert_ids, router_probs):
    tok_dev, width = hidden_out.shape
    experts = router_probs.shape[1]
    picked = jnp.take_along_axis(router_probs, expert_ids, axis=1)
    gate_w = picked / jnp.sum(picked, axis=1, keepdims=True)
    gated = (gate_w[:, :, None] * hidden_out[:, None, :].astype(jnp.float32)).astype(jnp.bfloat16)
    token_hits = jnp.sum((expert_ids[:, :, None] == jnp.arange(experts)).astype(jnp.int32), axis=1)
    earlier = jnp.cumsum(token_hits, axis=0) - token_hits
    slot_rank = jnp.take_along_axis(earlier, expert_ids, axis=1)
    send_buf = jnp.zeros((experts, tok_dev, width), jnp.bfloat16)
    return send_buf.at[expert_ids, slot_rank].set(gated, unique_indices=True)


def solution(mesh):
    group = mesh.shape['sp']
    row_spec = P(('dp', 'sp'), None)
    buf_spec = P(('dp', 'sp'), None, None)

    def device_step(x_loc, w_q, w_k, w_v, w_o, ids_loc, probs_loc):
        tok_dev = x_loc.shape[0]
        seq_len = tok_dev * group
        n_heads = w_q.shape[1] // HEAD_DIM
        kv_heads = w_k.shape[1] // HEAD_DIM
        kv_copies = max(1, group // kv_heads)
        head_dev = n_heads // group
        kv_dev = kv_heads * kv_copies // group
        q_loc = jnp.dot(x_loc, w_q, preferred_element_type=jnp.float32).astype(jnp.bfloat16).reshape(tok_dev, n_heads, HEAD_DIM)
        k_loc = jnp.dot(x_loc, w_k, preferred_element_type=jnp.float32).astype(jnp.bfloat16).reshape(tok_dev, kv_heads, HEAD_DIM)
        v_loc = jnp.dot(x_loc, w_v, preferred_element_type=jnp.float32).astype(jnp.bfloat16).reshape(tok_dev, kv_heads, HEAD_DIM)
        k_loc = jnp.repeat(k_loc, kv_copies, axis=1)
        v_loc = jnp.repeat(v_loc, kv_copies, axis=1)
        q_seq = lax.all_to_all(q_loc, 'sp', 1, 0, tiled=True)
        k_seq = lax.all_to_all(k_loc, 'sp', 1, 0, tiled=True)
        v_seq = lax.all_to_all(v_loc, 'sp', 1, 0, tiled=True)
        q_grp = q_seq.reshape(seq_len, kv_dev, head_dev // kv_dev, HEAD_DIM)
        scores = jnp.einsum('qgmd,kgd->gmqk', q_grp, k_seq, preferred_element_type=jnp.float32) * SCORE_SCALE
        positions = jnp.arange(seq_len)
        causal = positions[:, None] >= positions[None, :]
        weights = jax.nn.softmax(jnp.where(causal, scores, -1e30), axis=-1).astype(jnp.bfloat16)
        attn_seq = jnp.einsum('gmqk,kgd->qgmd', weights, v_seq, preferred_element_type=jnp.float32).astype(jnp.bfloat16)
        attn_seq = attn_seq.reshape(seq_len, head_dev, HEAD_DIM)
        attn_loc = lax.all_to_all(attn_seq, 'sp', 0, 1, tiled=True).reshape(tok_dev, n_heads * HEAD_DIM)
        out_proj = jnp.dot(attn_loc, w_o, preferred_element_type=jnp.float32)
        hidden_out = (x_loc.astype(jnp.float32) + out_proj).astype(jnp.bfloat16)
        send_buf = route_rows(hidden_out, ids_loc, probs_loc)
        recv_buf = lax.all_to_all(send_buf, 'sp', 0, 1, tiled=True)
        return hidden_out, recv_buf

    return jax.shard_map(device_step, mesh=mesh, in_specs=(row_spec, P(), P(), P(), P(), row_spec, row_spec), out_specs=(row_spec, buf_spec), check_vma=False)
```

profile of v0, /device:TPU:113, one launch (start us, length us, event | category | flops | bytes accessed | tf_op | source)
XLA Modules:
  0.0 802.1 jit_solution(588012791601079722)
XLA Ops:
  0.6 0.0 copy-start
  0.6 29.5 %fusion.11 = bf16[32,48,8,128]{3,2,1,0:T(8,128)(2,1)S(1)} fusion(bf16[256,6144]{1,0:T(8,128)(2,1)} %param.7, bf16[6144,6144]{1,0:T(8,128)(2,1)} %param.8), kind=kOutput, calls=%fused_computation.18 | convolution fusion | flops 19328925696 | bytes 81788928 | tf_op jit(solution)/shard_map/dot_general | solution.py:37
  30.2 2.5 copy.102
  32.7 6.0 all-to-all-start.2
  38.7 0.0 copy-start.1
  38.7 9.1 %fusion.13 = bf16[32,8,8,128]{3,2,1,0:T(8,128)(2,1)S(1)} fusion(bf16[256,6144]{1,0:T(8,128)(2,1)} %param.7, bf16[6144,1024]{1,0:T(8,128)(2,1)} %param.9), kind=kOutput, calls=%fused_computation.22 | convolution fusion | flops 3221487616 | bytes 16252928 | tf_op jit(solution)/shard_map/dot_general | solution.py:38
  47.8 0.9 copy.103
  48.7 0.0 copy-done.1
  48.7 6.6 fusion.12
  55.3 0.9 copy.104
  56.2 19.8 %all-to-all-done.2 = bf16[256,48,128]{2,0,1:T(8,128)(2,1)S(1)} async-done(((bf16[256,48,128]{2,0,1:T(8,128)(2,1)}), bf16[256,48,128]{2,0,1:T(8,128)(2,1)S(1)}, u32[]{:S(2)}, u32[]{:S(2)}) %all-to-all-start.2) | async-done | bytes 3145760 | tf_op jit(solution)/shard_map/all_to_all | solution.py:42
  76.0 5.2 all-to-all-start.1
  81.2 4.1 iota_compare_fusion
  85.3 1.9 copy.81
  87.2 3.3 all-to-all-done.1
  90.5 4.5 all-to-all-start
  95.0 38.3 %fusion.1 = (f32[6,2048]{1,0:T(8,128)S(1)}, f32[2048,2048,6]{1,0,2:T(8,128)}) fusion(pred[2048,2048]{0,1:T(8,128)(4,1)} %iota_compare_fusion, bf16[2048,128,1]{1,0,2:T(8,128)(2,1)} %bitcast.7, bf16[2048,6,128]{2,0,1:T(8,128)(2,1)} %bitcast.102), kind=kOutput, calls=%fused_computation.7 | convolution fusion | flops 6517936128 | bytes 108576768 | tf_op jit(solution)/shard_map/qgmd,kgd->gmqk/dot_general | solution.py:46
  133.3 35.2 %fusion = f32[6,2048]{1,0:T(8,128)S(1)} fusion(f32[2048,2048,6]{1,0,2:T(8,128)} %get-tuple-element.3, f32[6,2048]{1,0:T(8,128)S(1)} %get-tuple-element.2, pred[2048,2048]{0,1:T(8,128)(4,1)} %iota_compare_fusion), kind=kLoop, calls=%fused_computation.6 | loop fusion | flops 100651008 | bytes 104955904 | tf_op jit(solution)/shard_map/reduce_sum | solution.py:49
  168.5 0.0 all-to-all-done
  168.5 0.0 copy-start.2
  168.5 0.8 copy-done.2
  169.3 40.7 %fusion.8 = bf16[2048,6,128]{0,2,1:T(8,128)(2,1)S(1)} fusion(bf16[2048,128,1]{1,0,2:T(8,128)(2,1)} %bitcast.105, f32[6,2048]{1,0:T(8,128)S(1)} %fusion, f32[6,2048]{1,0:T(8,128)S(1)} %get-tuple-element.2, f32[2048,2048,6]{1,0,2:T(8,128)} %get-tuple-element.3, pred[2048,2048]{0,1:T(8,128)(4,1)} %iota_compare_fusion), kind=kOutput, calls=%fused_computation.17 | convolution fusion | flops 6569852928 | bytes 108625920 | tf_op jit(solution)/shard_map/gmqk,kgd->qgmd/dot_general | solution.py:50
  210.0 0.0 copy-start.3
  210.0 4.7 copy.83
  214.8 4.9 all-to-all-start.3
  219.7 0.0 copy-done.3
  219.7 0.1 copy.88
  219.8 0.1 reshape.96
  220.0 0.0 copy-done
  220.0 3.5 gather_fusion.1
  223.5 0.1 reshape.105
  223.6 0.1 copy.91
  223.8 0.1 copy.92
  223.9 0.1 copy.87
  224.1 0.6 reduce-window.6
  224.6 0.2 slice_reduce_fusion
  224.9 0.1 add_bitcast_fusion
  225.0 0.1 copy.86
  225.1 3.8 gather_fusion
  228.9 0.1 reshape.99
  229.1 0.1 copy.89
  229.2 0.1 copy.90
  229.3 0.1 reshape.108
  229.5 38.9 %all-to-all-done.3 = bf16[2048,6,128]{2,1,0:T(8,128)(2,1)} async-done(((bf16[2048,6,128]{2,1,0:T(8,128)(2,1)}), bf16[2048,6,128]{2,1,0:T(8,128)(2,1)}, u32[]{:S(2)}, u32[]{:S(2)}) %all-to-all-start.3) | async-done | bytes 3145760 | tf_op jit(solution)/shard_map/all_to_all | solution.py:52
  268.4 5.7 copy.85
  274.1 34.3 %fusion.20 = (f32[256,6144]{1,0:T(8,128)}, bf16[256,6144]{1,0:T(8,128)(2,1)}) fusion(bf16[256,6144]{0,1:T(8,128)(2,1)S(1)} %bitcast.99, bf16[6144,6144]{1,0:T(8,128)(2,1)} %param.11, bf16[256,6144]{1,0:T(8,128)(2,1)} %param.7), kind=kOutput, calls=%fused_computation.45 | convolution fusion | flops 19333644288 | bytes 91226112 | tf_op jit(solution)/shard_map/dot_general | solution.py:53
  308.4 8.5 %multiply_convert_fusion = bf16[256,2,6144]{2,1,0:T(2,128)(2,1)} fusion(f32[256,6144]{1,0:T(8,128)} %get-tuple-element.4, f32[256,2]{1,0:T(8,128)S(1)} %copy.92), kind=kLoop, calls=%fused_computation.11 | loop fusion | flops 6291456 | bytes 12584960 | tf_op jit(solution)/shard_map/convert_element_type | solution.py:16
  316.9 13.3 %reshape.110 = bf16[512,6144]{1,0:T(8,128)(2,1)} reshape(bf16[256,2,6144]{2,1,0:T(2,128)(2,1)} %multiply_convert_fusion) | data formatting | bytes 12582912 | tf_op jit(solution)/shard_map/convert_element_type | solution.py:16
  330.2 8.6 %broadcast_in_dim.34 = bf16[8,256,6144]{2,1,0:T(8,128)(2,1)} broadcast(bf16[]{:T(256)} %constant.25.clone.1), dimensions={} | broadcast | bytes 25165826 | tf_op jit(solution)/shard_map/broadcast_in_dim | solution.py:20
  338.9 174.6 %scatter_fusion = bf16[8,256,6144]{2,1,0:T(8,128)(2,1)} fusion(bf16[8,256,6144]{2,1,0:T(8,128)(2,1)} %broadcast_in_dim.34, s32[512]{0:T(512)S(1)} %reshape.108, bf16[512,6144]{1,0:T(8,128)(2,1)} %reshape.110), kind=kCustom, calls=%fused_computation.2 | custom fusion | bytes 18878464 | tf_op jit(solution)/shard_map/scatter | solution.py:21
  513.5 279.8 %all_to_all.72 = bf16[8,256,6144]{2,1,0:T(8,128)(2,1)S(1)} all-to-all(bf16[8,256,6144]{2,1,0:T(8,128)(2,1)} %scatter_fusion), channel_id=1, replica_groups=mesh['dp'=2,'sp'=8] {'sp'}, dimensions={0} | all-to-all | bytes 50331648 | tf_op jit(solution)/shard_map/all_to_all | solution.py:56
  793.2 8.9 %copy.107 = bf16[1,2048,6144]{2,1,0:T(8,128)(2,1)} copy(bf16[1,2048,6144]{2,1,0:T(8,128)(2,1)S(1)} %bitcast.98) | data formatting | bytes 50331648
  (8 shorter events, 0.1 us)
Async XLA Ops:
  0.6 219.4 %copy-start = (f32[256,8]{0,1:T(8,128)S(1)}, f32[256,8]{0,1:T(8,128)}, u32[]{:S(2)}) copy-start(f32[256,8]{0,1:T(8,128)} %param.13) | copy-start | bytes 24580
  32.7 43.2 %all-to-all-start.2 = ((bf16[256,48,128]{2,0,1:T(8,128)(2,1)}), bf16[256,48,128]{2,0,1:T(8,128)(2,1)S(1)}, u32[]{:S(2)}, u32[]{:S(2)}) async-start(bf16[256,48,128]{2,0,1:T(8,128)(2,1)} %bitcast.101), calls=%async_computation.2 | async-start | bytes 6291456 | tf_op jit(solution)/shard_map/all_to_all | solution.py:42
  38.7 10.0 %copy-start.1 = (bf16[256,6144]{1,0:T(8,128)(2,1)S(1)}, bf16[256,6144]{1,0:T(8,128)(2,1)}, u32[]{:S(2)}) copy-start(bf16[256,6144]{1,0:T(8,128)(2,1)} %param.7) | copy-start | bytes 9437188
  76.0 14.6 %all-to-all-start.1 = ((bf16[256,8,128]{2,0,1:T(8,128)(2,1)}), bf16[256,8,128]{2,0,1:T(8,128)(2,1)}, u32[]{:S(2)}, u32[]{:S(2)}) async-start(bf16[256,8,128]{2,0,1:T(8,128)(2,1)} %bitcast.104), calls=%async_computation.1 | async-start | bytes 1048576 | tf_op jit(solution)/shard_map/all_to_all | solution.py:43
  90.5 78.0 %all-to-all-start = ((bf16[256,8,128]{2,0,1:T(8,128)(2,1)}), bf16[256,8,128]{2,0,1:T(8,128)(2,1)S(1)}, u32[]{:S(2)}, u32[]{:S(2)}) async-start(bf16[256,8,128]{2,0,1:T(8,128)(2,1)} %bitcast.103), calls=%async_computation | async-start | bytes 1048576 | tf_op jit(solution)/shard_map/all_to_all | solution.py:44
  168.5 0.8 copy-start.2
  210.0 9.7 %copy-start.3 = (s32[256,2]{0,1:T(2,128)S(1)}, s32[256,2]{0,1:T(2,128)}, u32[]{:S(2)}) copy-start(s32[256,2]{0,1:T(2,128)} %param.12) | copy-start | bytes 6148
  214.8 53.6 %all-to-all-start.3 = ((bf16[2048,6,128]{2,1,0:T(8,128)(2,1)}), bf16[2048,6,128]{2,1,0:T(8,128)(2,1)}, u32[]{:S(2)}, u32[]{:S(2)}) async-start(bf16[2048,6,128]{2,1,0:T(8,128)(2,1)} %copy.83), calls=%async_computation.3 | async-start | bytes 8388608 | tf_op jit(solution)/shard_map/all_to_all | solution.py:52
where the time goes:
time: 805 us; the launch traced here: 802 us
  blocking collectives  280 us (35%)
  local copies, waits for them, and re-layouts  232 us (29%)
  matrix products  158 us (20%)
  waiting for transfers between devices  62 us (8%)
  other arithmetic  48.6 us (6%)
  starting transfers between devices  20.6 us (3%)
    all_to_all x1, blocking collectives, device_step(): recv_buf = lax.all_to_all(send_buf, 'sp', 0, 1, tiled=True)  280 us
    scatter x1, local copies, waits for them, and re-layouts, route_rows(): return send_buf.at[expert_ids, slot_rank].set(gated, unique_indices=True)  175 us
    dot_general x1, matrix products, device_step(): jnp.einsum('gmqk,kgd->qgmd', weights, v_seq, preferred_element_type=jnp.f...  40.7 us
    all_to_all x1, waiting for transfers between devices, device_step(): lax.all_to_all(attn_seq, 'sp', 0, 1, tiled=True)  38.9 us
    dot_general x1, matrix products, device_step(): jnp.einsum('qgmd,kgd->gmqk', q_grp, k_seq, preferred_element_type=jnp.flo...  38.3 us
    reduce_sum x1, other arithmetic, device_step(): jax.nn.softmax(jnp.where(causal, scores, -1e+30), axis=-1)  35.2 us
    dot_general x1, matrix products, device_step(): out_proj = jnp.dot(attn_loc, w_o, preferred_element_type=jnp.float32)  34.3 us
    dot_general x1, matrix products, device_step(): jnp.dot(x_loc, w_q, preferred_element_type=jnp.float32).astype(jnp.bfloat16)  29.5 us
  transfers between devices with their start and end apart: 4, of which 3 were waited for; matrix products, arithmetic and copies ran while one was open for 13% of the time, Pallas kernels for 0%

commit v1 on v0

v1 whole, which is shorter than its diff:
```python
import functools
import math
import jax
import jax.numpy as jnp
from jax import lax
from jax.experimental import pallas as pl
from jax.experimental.pallas import tpu as pltpu
from jax.sharding import PartitionSpec as P

HEAD = 128
SCALE = 1.0 / math.sqrt(HEAD)
NEG = -1e30
WIDE = 512
CHUNKS = 4


def attn_kernel(q_ref, k_ref, v_ref, o_ref, m_ref, l_ref, acc_ref):
    me = lax.axis_index('sp')
    rows, width = q_ref.shape
    heads = width // HEAD

    def block(start, size, masked, first):
        k_blk = k_ref[pl.ds(start, size), :]
        v_blk = v_ref[pl.ds(start, size), :]
        for h in range(heads):
            q_h = q_ref[:, h * HEAD:(h + 1) * HEAD]
            s = lax.dot_general(q_h, k_blk, (((1,), (1,)), ((), ())), preferred_element_type=jnp.float32) * SCALE
            if masked:
                r = lax.broadcasted_iota(jnp.int32, s.shape, 0)
                c = lax.broadcasted_iota(jnp.int32, s.shape, 1)
                s = jnp.where(r >= c, s, NEG)
            m_blk = jnp.max(s, axis=1, keepdims=True)
            if first:
                m_new = m_blk
                p = jnp.exp(s - m_new)
                l_ref[h] = jnp.broadcast_to(jnp.sum(p, axis=1, keepdims=True), (rows, HEAD))
                acc_ref[h] = jnp.dot(p.astype(jnp.bfloat16), v_blk, preferred_element_type=jnp.float32)
            else:
                m_old = m_ref[h][:, :1]
                m_new = jnp.maximum(m_old, m_blk)
                p = jnp.exp(s - m_new)
                a = jnp.exp(m_old - m_new)
                l_ref[h] = l_ref[h] * a + jnp.broadcast_to(jnp.sum(p, axis=1, keepdims=True), (rows, HEAD))
                acc_ref[h] = acc_ref[h] * a + jnp.dot(p.astype(jnp.bfloat16), v_blk, preferred_element_type=jnp.float32)
            m_ref[h] = jnp.broadcast_to(m_new, (rows, HEAD))

    block(pl.multiple_of(me * rows, rows), rows, True, True)
    odd = lax.rem(me * rows, WIDE) // rows

    @pl.when(odd == 1)
    def _():
        block(0, rows, False, False)

    @pl.loop(0, (me * rows) // WIDE)
    def _(j):
        block(pl.multiple_of(odd * rows + j * WIDE, rows), WIDE, False, False)

    for h in range(heads):
        o_ref[:, h * HEAD:(h + 1) * HEAD] = (acc_ref[h] / l_ref[h]).astype(o_ref.dtype)


def route_kernel(slot_ref, gate_ref, *refs):
    *h_refs, out_ref = refs
    rows = out_ref.shape[0]
    slot = slot_ref[0]
    r = lax.broadcasted_iota(jnp.int32, (rows, rows), 0)
    pick = slot.astype(jnp.int32) == r
    gate = jnp.sum(jnp.where(pick, gate_ref[0], 0.0), axis=1, keepdims=True)
    pick = jnp.where(pick, 1.0, 0.0).astype(jnp.bfloat16)
    off = 0
    for h_ref in h_refs:
        wid = h_ref.shape[1]
        got = jnp.dot(pick, h_ref[...], preferred_element_type=jnp.float32)
        out_ref[:, off:off + wid] = (gate * got).astype(out_ref.dtype)
        off += wid


def solution(mesh):
    group = mesh.shape['sp']
    row_spec = P(('dp', 'sp'), None)
    buf_spec = P(('dp', 'sp'), None, None)

    def step(x, w_q, w_k, w_v, w_o, ids, probs):
        rows, width = x.shape
        seq = rows * group
        kv_w = w_k.shape[1]
        kv_heads = kv_w // HEAD
        q_w = w_q.shape[1]
        per = q_w // kv_heads
        experts = probs.shape[1]
        hit = jnp.any(ids[:, :, None] == jnp.arange(experts), axis=1)
        picked = jnp.where(hit, probs, 0.0)
        gate = picked / jnp.sum(picked, axis=1, keepdims=True)
        hits = hit.astype(jnp.bfloat16)
        tri = (jnp.arange(rows)[:, None] > jnp.arange(rows)[None, :]).astype(jnp.bfloat16)
        slot = jnp.where(hit, jnp.dot(tri, hits, preferred_element_type=jnp.float32), -1.0)
        table = jnp.stack([slot.T, gate.T], axis=1)
        table = lax.all_to_all(table, 'sp', 0, 0, tiled=True)
        slot_e = table[:, 0:1, :]
        gate_e = table[:, 1:2, :]

        k = jnp.dot(x, w_k, preferred_element_type=jnp.float32).astype(jnp.bfloat16)
        v = jnp.dot(x, w_v, preferred_element_type=jnp.float32).astype(jnp.bfloat16)
        kv = lax.all_gather(jnp.concatenate([k, v], axis=1), 'sp', axis=0, tiled=True)
        q = jnp.dot(x, w_q, preferred_element_type=jnp.float32).astype(jnp.bfloat16)
        o = pl.pallas_call(
            attn_kernel,
            grid=(kv_heads,),
            in_specs=[
                pl.BlockSpec((rows, per), lambda g: (0, g)),
                pl.BlockSpec((seq, HEAD), lambda g: (0, g)),
                pl.BlockSpec((seq, HEAD), lambda g: (0, kv_heads + g)),
            ],
            out_specs=pl.BlockSpec((rows, per), lambda g: (0, g)),
            out_shape=jax.ShapeDtypeStruct((rows, q_w), jnp.bfloat16),
            scratch_shapes=[pltpu.VMEM((per // HEAD, rows, HEAD), jnp.float32)] * 3,
        )(q, kv, kv)
        wid = width // CHUNKS
        parts, gathered = [], []
        for c in range(CHUNKS):
            cols = slice(c * wid, (c + 1) * wid)
            y = jnp.dot(o, w_o[:, cols], preferred_element_type=jnp.float32)
            h_c = (x[:, cols].astype(jnp.float32) + y).astype(jnp.bfloat16)
            parts.append(h_c)
            gathered.append(lax.all_gather(h_c, 'sp', axis=0, tiled=True))
        hidden_out = jnp.concatenate(parts, axis=1)
        buf = pl.pallas_call(
            route_kernel,
            grid=(group,),
            in_specs=[pl.BlockSpec((1, 1, rows), lambda s: (s, 0, 0))] * 2 + [pl.BlockSpec((rows, wid), lambda s: (s, 0))] * CHUNKS,
            out_specs=pl.BlockSpec((rows, width), lambda s: (s, 0)),
            out_shape=jax.ShapeDtypeStruct((seq, width), jnp.bfloat16),
        )(slot_e, gate_e, *gathered)
        return hidden_out, buf[None]

    return jax.shard_map(step, mesh=mesh, in_specs=(row_spec, P(), P(), P(), P(), row_spec, row_spec), out_specs=(row_spec, buf_spec), check_vma=False)
```

time: 805 us -> 361 us (0.45)
  local copies, waits for them, and re-layouts: 232 us -> 1.56 us
  blocking collectives: 280 us -> 72.5 us
  matrix products: 158 us -> 85.6 us
  waiting for transfers between devices: 62 us -> 126 us
  Pallas kernels: 0 us -> 56 us
  other arithmetic: 48.6 us -> 3.96 us
  starting transfers between devices: 20.6 us -> 0.72 us
  between operations: 0.85 us -> 13.9 us
    all_to_all x1, blocking collectives: 280 us -> 72.5 us  [step(): table = lax.all_to_all(table, 'sp', 0, 0, tiled=True)]
    scatter x1 -> x0, local copies, waits for them, and re-layouts: 175 us -> none  [route_rows(): return send_buf.at[expert_ids, slot_rank].set(gated, unique_indices=True)]
    all_gather x0 -> x5, waiting for transfers between devices: none -> 126 us  [the longest x4 108 us: step(): gathered.append(lax.all_gather(h_c, 'sp', axis=0, tiled=True))]
    dot_general x6 -> x8, matrix products: 158 us -> 85.6 us  [the longest x4 42.2 us: step(): y = jnp.dot(o, w_o[:, cols], preferred_element_type=jnp.float32)]
    all_to_all x4 -> x0, waiting for transfers between devices: 62 us -> none  [the longest x1 38.9 us: device_step(): lax.all_to_all(attn_seq, 'sp', 0, 1, tiled=True)]
    pallas_call x0 -> x2, Pallas kernels: none -> 56 us  [the longest x1 35.1 us: step(): pl.pallas_call(attn_kernel, grid=(kv_heads,), in_specs=[pl.BlockSpec((row...]
    reduce_sum x3 -> x1, other arithmetic: 35.2 us -> 0.02 us  [step(): gate = picked / jnp.sum(picked, axis=1, keepdims=True)]
    all_to_all x4 -> x0, starting transfers between devices: 20.6 us -> none  [the longest x1 6.01 us: device_step(): q_seq = lax.all_to_all(q_loc, 'sp', 1, 0, tiled=True)]
  transfers between devices with their start and end apart: 4 -> 5, of which waited for: 3 -> 4; matrix products, arithmetic and copies ran while one was open for 13% -> 18% of each run, Pallas kernels for 0% -> 0%
where the time goes in v1:
time: 361 us
  waiting for transfers between devices  126 us (35%)
  matrix products  85.6 us (24%)
  blocking collectives  72.5 us (20%)
  Pallas kernels  56 us (16%)
  between operations  13.9 us (4%)
  other arithmetic  3.96 us (1%)
    all_gather x4, waiting for transfers between devices, step(): gathered.append(lax.all_gather(h_c, 'sp', axis=0, tiled=True))  108 us
    all_to_all x1, blocking collectives, step(): table = lax.all_to_all(table, 'sp', 0, 0, tiled=True)  72.5 us
    dot_general x4, matrix products, step(): y = jnp.dot(o, w_o[:, cols], preferred_element_type=jnp.float32)  42.2 us
    pallas_call x1, Pallas kernels, step(): pl.pallas_call(attn_kernel, grid=(kv_heads,), in_specs=[pl.BlockSpec((row...  35.1 us
    dot_general x1, matrix products, step(): q = jnp.dot(x, w_q, preferred_element_type=jnp.float32).astype(jnp.bfloat16)  30.6 us
    pallas_call x1, Pallas kernels, step(): pl.pallas_call(route_kernel, grid=(group,), in_specs=[pl.BlockSpec((1, 1,...  20.9 us
    all_gather x1, waiting for transfers between devices, step(): lax.all_gather(jnp.concatenate([k, v], axis=1), 'sp', axis=0, tiled=True)  18 us
    dot_general x1, matrix products, step(): k = jnp.dot(x, w_k, preferred_element_type=jnp.float32).astype(jnp.bfloat16)  9.08 us
  transfers between devices with their start and end apart: 5, of which 4 were waited for; matrix products, arithmetic and copies ran while one was open for 18% of the time, Pallas kernels for 0%

profile of v1, /device:TPU:113, one launch (start us, length us, event | category | flops | bytes accessed | tf_op | source)
XLA Modules:
  0.0 360.6 jit_solution(1307974297957387012)
XLA Ops:
  7.2 0.0 copy-start.7
  7.2 0.1 all-gather.6.cloned.1.call-start
  7.3 0.0 copy-start.6
  7.3 9.1 %convolution_convert_fusion.2 = bf16[256,1024]{1,0:T(8,128)(2,1)S(1)} fusion(bf16[256,6144]{1,0:T(8,128)(2,1)} %param.7, bf16[6144,1024]{1,0:T(8,128)(2,1)} %param.9), kind=kOutput, calls=%fused_computation.19 | convolution fusion | flops 3221487616 | bytes 16252928 | tf_op jit(solution)/shard_map/dot_general | solution.py:102
  16.4 0.0 copy-done.7
  16.4 0.9 copy-done.6
  17.3 3.5 convolution_convert_fusion.1
  20.8 1.1 pad_maximum_fusion.1
  21.9 0.1 all-gather.6.cloned.1.call-update
  21.9 0.2 all-gather.14.cloned.1.call-start
  22.2 30.6 %convolution_convert_fusion.q_ref = bf16[256,6144]{1,0:T(8,128)(2,1)} fusion(bf16[256,6144]{1,0:T(8,128)(2,1)S(1)} %copy-done.7, bf16[6144,6144]{1,0:T(8,128)(2,1)} %param.8), kind=kOutput, calls=%fused_computation.8 | convolution fusion | flops 19328925696 | bytes 81788928 | tf_op jit(solution)/shard_map/dot_general | solution.py:105
  52.8 18.0 %all-gather.6.cloned.1.call-done.k_ref.v_ref = bf16[2048,2048]{1,0:T(8,128)(2,1)} async-done(((bf16[256,2048]{1,0:T(8,128)(2,1)}), bf16[2048,2048]{1,0:T(8,128)(2,1)}) %all-gather.6.cloned.1.call-update) | async-done | bytes 8388624 | tf_op jit(solution)/shard_map/all_gather | solution.py:104
  70.8 35.1 %shard_map.86 = bf16[256,6144]{1,0:T(8,128)(2,1)} custom-call(bf16[256,6144]{1,0:T(8,128)(2,1)} %convolution_convert_fusion.q_ref, bf16[2048,2048]{1,0:T(8,128)(2,1)} %all-gather.6.cloned.1.call-done.k_ref.v_ref, bf16[2048,2048]{1,0:T(8,128)(2,1)} %all-gather.6.cloned.1.call-done.k_ref.v_ref), custom_call_target="tpu_custom_call" | custom-call | tf_op jit(solution)/shard_map/pallas_call | solution.py:106
  105.9 0.0 copy-start.3
  105.9 11.0 %fusion.20 = bf16[256,1536]{1,0:T(8,128)(2,1)} fusion(bf16[256,6144]{1,0:T(8,128)(2,1)} %shard_map.86, bf16[6144,6144]{1,0:T(8,128)(2,1)} %param.11, bf16[256,6144]{1,0:T(8,128)(2,1)} %param.7), kind=kOutput, calls=%fused_computation.14 | convolution fusion | flops 4833017856 | bytes 23592960 | tf_op jit(solution)/shard_map/dot_general | solution.py:122
  116.9 0.1 all-gather.14.cloned.1.call-update
  117.0 0.3 all-gather.12.cloned.1.call-start
  117.2 0.0 copy-done.3
  117.3 10.1 %fusion.23 = bf16[256,1536]{1,0:T(8,128)(2,1)} fusion(bf16[256,6144]{1,0:T(8,128)(2,1)S(1)} %copy-done.3, bf16[6144,6144]{1,0:T(8,128)(2,1)} %param.11, bf16[256,6144]{1,0:T(8,128)(2,1)} %param.7), kind=kOutput, calls=%fused_computation.15 | convolution fusion | flops 4833017856 | bytes 23592960 | tf_op jit(solution)/shard_map/dot_general | solution.py:122
  127.4 0.1 all-gather.12.cloned.1.call-update
  127.4 0.1 all-gather.8.cloned.1.call-start
  127.5 10.0 %fusion.29 = bf16[256,1536]{1,0:T(8,128)(2,1)} fusion(bf16[256,6144]{1,0:T(8,128)(2,1)S(1)} %copy-done.3, bf16[6144,6144]{1,0:T(8,128)(2,1)} %param.11, bf16[256,6144]{1,0:T(8,128)(2,1)} %param.7), kind=kOutput, calls=%fused_computation.17 | convolution fusion | flops 4833017856 | bytes 23592960 | tf_op jit(solution)/shard_map/dot_general | solution.py:122
  137.5 0.1 all-gather.8.cloned.1.call-update
  137.5 0.0 copy-start.5
  137.5 0.0 copy-start.4
  137.5 0.0 copy-start
  137.6 0.0 copy-start.1
  137.6 0.0 copy-start.2
  137.6 0.1 all-gather.10.cloned.1.call-start
  137.6 11.2 %fusion.26 = bf16[256,1536]{1,0:T(8,128)(2,1)} fusion(bf16[256,6144]{1,0:T(8,128)(2,1)} %shard_map.86, bf16[6144,6144]{1,0:T(8,128)(2,1)} %param.11, bf16[256,6144]{1,0:T(8,128)(2,1)} %param.7), kind=kOutput, calls=%fused_computation.16 | convolution fusion | flops 4833017856 | bytes 23592960 | tf_op jit(solution)/shard_map/dot_general | solution.py:122
  148.8 0.1 all-gather.10.cloned.1.call-update
  148.9 0.0 copy-done.5
  148.9 0.0 copy-done.4
  149.0 0.2 convolution_select_fusion
  149.2 72.5 %all_to_all.5 = f32[8,2,256]{2,1,0:T(2,128)S(1)} all-to-all(f32[8,2,256]{2,1,0:T(2,128)S(1)} %pad_maximum_fusion.2), channel_id=1, replica_groups=mesh['dp'=2,'sp'=8] {'sp'}, dimensions={0} | all-to-all | bytes 32768 | tf_op jit(solution)/shard_map/all_to_all | solution.py:98
  221.7 0.6 fusion.34
  222.3 0.0 copy-done
  222.3 0.0 copy-done.1
  222.3 0.0 copy-done.2
  222.3 2.8 pad_maximum_fusion
  225.1 0.0 all-gather.14.cloned.1.call-done.refs_3_
  225.1 31.7 %all-gather.12.cloned.1.call-done.refs_2_ = bf16[2048,1536]{1,0:T(8,128)(2,1)} async-done(((bf16[256,1536]{1,0:T(8,128)(2,1)}), bf16[2048,1536]{1,0:T(8,128)(2,1)}) %all-gather.12.cloned.1.call-update) | async-done | bytes 6291472 | tf_op jit(solution)/shard_map/all_gather | solution.py:125
  256.9 38.1 %all-gather.8.cloned.1.call-done.refs_0_ = bf16[2048,1536]{1,0:T(8,128)(2,1)} async-done(((bf16[256,1536]{1,0:T(8,128)(2,1)}), bf16[2048,1536]{1,0:T(8,128)(2,1)}) %all-gather.8.cloned.1.call-update) | async-done | bytes 6291472 | tf_op jit(solution)/shard_map/all_gather | solution.py:125
  295.0 38.1 %all-gather.10.cloned.1.call-done.refs_1_ = bf16[2048,1536]{1,0:T(8,128)(2,1)} async-done(((bf16[256,1536]{1,0:T(8,128)(2,1)}), bf16[2048,1536]{1,0:T(8,128)(2,1)}) %all-gather.10.cloned.1.call-update) | async-done | bytes 6291472 | tf_op jit(solution)/shard_map/all_gather | solution.py:125
  333.1 20.9 %shard_map.87 = bf16[2048,6144]{1,0:T(8,128)(2,1)} custom-call(f32[8,1,256]{2,1,0:T(1,128)} %get-tuple-element.3.slot_ref, f32[8,1,256]{2,1,0:T(1,128)} %get-tuple-element.2.gate_ref, bf16[2048,1536]{1,0:T(8,128)(2,1)} %all-gather.8.cloned.1.call-done.refs_0_, bf16[2048,1536]{1,0:T(8,128)(2,1)} %all-gather.10.cloned.1.call-done.refs_1_, ...), custom_call_target="tpu_custom_call" | custom-call | tf_op jit(solution)/shard_map/pallas_call | solution.py:127
  (6 shorter events, 0.1 us)
Async XLA Ops:
  7.2 9.2 %copy-start.7 = (bf16[256,6144]{1,0:T(8,128)(2,1)S(1)}, bf16[256,6144]{1,0:T(8,128)(2,1)}, u32[]{:S(2)}) copy-start(bf16[256,6144]{1,0:T(8,128)(2,1)} %param.7) | copy-start | bytes 9437188
  7.2 63.6 %all-gather.6.cloned.1.call-start = ((), (), s32[]{:S(2)}) async-start(), calls=%async_computation.1 | async-start | bytes 9437184 | tf_op jit(solution)/shard_map/all_gather | solution.py:104
  7.3 10.0 %copy-start.6 = (bf16[6144,1024]{1,0:T(8,128)(2,1)S(1)}, bf16[6144,1024]{1,0:T(8,128)(2,1)}, u32[]{:S(2)}) copy-start(bf16[6144,1024]{1,0:T(8,128)(2,1)} %param.10) | copy-start | bytes 37748740
  21.9 203.2 %all-gather.14.cloned.1.call-start = ((), (), s32[]{:S(2)}) async-start(), calls=%async_computation.5 | async-start | bytes 7077888 | tf_op jit(solution)/shard_map/all_gather | solution.py:125
  105.9 11.4 %copy-start.3 = (bf16[256,6144]{1,0:T(8,128)(2,1)S(1)}, bf16[256,6144]{1,0:T(8,128)(2,1)}, u32[]{:S(2)}) copy-start(bf16[256,6144]{1,0:T(8,128)(2,1)} %shard_map.86) | copy-start | bytes 9437188
  117.0 139.9 %all-gather.12.cloned.1.call-start = ((), (), s32[]{:S(2)}) async-start(), calls=%async_computation.4 | async-start | bytes 7077888 | tf_op jit(solution)/shard_map/all_gather | solution.py:125
  127.4 167.6 %all-gather.8.cloned.1.call-start = ((), (), s32[]{:S(2)}) async-start(), calls=%async_computation.2 | async-start | bytes 7077888 | tf_op jit(solution)/shard_map/all_gather | solution.py:125
  137.5 11.4 %copy-start.5 = (s32[256,2]{0,1:T(2,128)S(1)}, s32[256,2]{0,1:T(2,128)}, u32[]{:S(2)}) copy-start(s32[256,2]{0,1:T(2,128)} %param.12) | copy-start | bytes 6148
  137.5 11.4 %copy-start.4 = (f32[256,8]{0,1:T(8,128)S(1)}, f32[256,8]{0,1:T(8,128)}, u32[]{:S(2)}) copy-start(f32[256,8]{0,1:T(8,128)} %param.13) | copy-start | bytes 24580
  137.5 84.8 %copy-start = (bf16[256,1536]{1,0:T(8,128)(2,1)S(1)}, bf16[256,1536]{1,0:T(8,128)(2,1)}, u32[]{:S(2)}) copy-start(bf16[256,1536]{1,0:T(8,128)(2,1)} %fusion.20) | copy-start | bytes 2359300
  137.6 84.8 %copy-start.1 = (bf16[256,1536]{1,0:T(8,128)(2,1)S(1)}, bf16[256,1536]{1,0:T(8,128)(2,1)}, u32[]{:S(2)}) copy-start(bf16[256,1536]{1,0:T(8,128)(2,1)} %fusion.23) | copy-start | bytes 2359300
  137.6 84.7 %copy-start.2 = (bf16[256,1536]{1,0:T(8,128)(2,1)S(1)}, bf16[256,1536]{1,0:T(8,128)(2,1)}, u32[]{:S(2)}) copy-start(bf16[256,1536]{1,0:T(8,128)(2,1)} %fusion.29) | copy-start | bytes 2359300
  137.6 195.5 %all-gather.10.cloned.1.call-start = ((), (), s32[]{:S(2)}) async-start(), calls=%async_computation.3 | async-start | bytes 7077888 | tf_op jit(solution)/shard_map/all_gather | solution.py:125
Sparse Core Ops, SparseCore 0:
  22.0 48.7 all-gather.5
  117.1 101.4 all-gather.13
  220.2 36.6 all-gather.11
  258.3 36.6 all-gather.7
  296.4 36.6 all-gather.9

commit v2 on v0

v2 whole, which is shorter than its diff:
```python
import functools
import math
import jax
import jax.numpy as jnp
from jax import lax
from jax.experimental import pallas as pl
from jax.experimental.pallas import tpu as pltpu
from jax.sharding import PartitionSpec as P

HEAD = 128
LOG_SCALE = math.log2(math.e) / math.sqrt(HEAD)
NEG = -1e30
CW = 2 * HEAD
DEPTH = 3
BF16 = jnp.bfloat16
F32 = jnp.float32
MESH = pl.DeviceIdType.MESH


def block_kernel(group, x_ref, wq_ref, wk_ref, wv_ref, wo_ref, tab_ref, h_ref, tabs_ref,
                 q_ref, o_ref, kv_ref, w_ref, m_ref, l_ref, acc_ref,
                 w_sem, x_sem, xs_sem, xr_sem, kvs_sem, kvr_sem, kvf_sem, os_sem, or_sem,
                 hs_sem, hf_sem, hrel_sem, hr_sem, ts_sem, tr_sem):
    me = lax.axis_index('sp')
    chips = group // 2
    chip, core = me // 2, lax.rem(me, 2)
    rows = x_ref.shape[0]
    n_col = x_ref.shape[1] // CW
    half = n_col // 2
    n_kv = wk_ref.shape[1] // HEAD // 2
    per = half // n_kv
    mine = core * half
    sib = chip * 2 + (1 - core)
    right = lax.rem(chip + 1, chips)
    left = lax.rem(chip + chips - 1, chips)
    opp = lax.rem(chip + 2, chips)

    def lane(c):
        return {'sp': c * 2 + core}

    def remote(src, dst, send, recv, dev):
        return pltpu.make_async_remote_copy(src_ref=src, dst_ref=dst, send_sem=send, recv_sem=recv, device_id=dev, device_id_type=MESH)

    n_w = n_kv + 2 * half

    def w_start(i, stage):
        slot = lax.rem(i, DEPTH)
        if stage == 'kv':
            col = pl.multiple_of((core * n_kv + i) * HEAD, HEAD)
            pltpu.make_async_copy(wk_ref.at[:, pl.ds(col, HEAD)], w_ref.at[slot, :, pl.ds(0, HEAD)], w_sem.at[slot, 0]).start()
            pltpu.make_async_copy(wv_ref.at[:, pl.ds(col, HEAD)], w_ref.at[slot, :, pl.ds(HEAD, HEAD)], w_sem.at[slot, 1]).start()
        else:
            src = wq_ref if stage == 'q' else wo_ref
            j = i - n_kv if stage == 'q' else i - n_kv - half
            col = pl.multiple_of((mine + j) * CW, CW)
            pltpu.make_async_copy(src.at[:, pl.ds(col, CW)], w_ref.at[slot], w_sem.at[slot, 0]).start()

    def w_wait(i, stage):
        slot = lax.rem(i, DEPTH)
        if stage == 'kv':
            pltpu.make_async_copy(wk_ref.at[:, pl.ds(0, HEAD)], w_ref.at[slot, :, pl.ds(0, HEAD)], w_sem.at[slot, 0]).wait()
            pltpu.make_async_copy(wv_ref.at[:, pl.ds(0, HEAD)], w_ref.at[slot, :, pl.ds(HEAD, HEAD)], w_sem.at[slot, 1]).wait()
        else:
            pltpu.make_async_copy(wq_ref.at[:, pl.ds(0, CW)], w_ref.at[slot], w_sem.at[slot, 0]).wait()
        return slot

    own_rows = pl.ds(pl.multiple_of(core * rows, rows), rows)
    for j in range(n_col):
        pltpu.make_async_copy(x_ref.at[:, pl.ds(j * CW, CW)], h_ref.at[chip, j, own_rows], x_sem.at[j]).start()
    for i in range(DEPTH):
        w_start(i, 'kv')

    barrier = pltpu.get_barrier_semaphore()
    for d in range(1, group):
        pl.semaphore_signal(barrier, inc=1, device_id={'sp': lax.rem(me + d, group)}, device_id_type=MESH)
    pl.semaphore_wait(barrier, group - 1)

    for j in range(n_col):
        pltpu.make_async_copy(x_ref.at[:, pl.ds(j * CW, CW)], h_ref.at[chip, j, own_rows], x_sem.at[j]).wait()
    x_copy = remote(h_ref.at[chip, :, own_rows], h_ref.at[chip, :, own_rows], xs_sem, xr_sem, {'sp': sib})
    x_copy.start()
    tab_own = pltpu.make_async_copy(tab_ref, tabs_ref.at[me], ts_sem.at[0])
    tab_own.start()
    tab_copies = []
    for d in range(1, group):
        cp = remote(tab_ref, tabs_ref.at[me], ts_sem.at[d], tr_sem.at[d], {'sp': lax.rem(me + d, group)})
        cp.start()
        tab_copies.append(cp)
    x_copy.wait_recv()

    def product(lhs_ref, base, slot):
        lhs = jnp.concatenate([lhs_ref[base, j] for j in range(n_col)], axis=1)
        return jnp.dot(lhs, w_ref[slot], preferred_element_type=F32)

    def kv_own(g, to):
        s = 0 if to == 'r' else 1
        return remote(kv_ref.at[chip, g], kv_ref.at[chip, g], kvs_sem.at[s, g], kvr_sem.at[chip, g], lane(right if to == 'r' else left))

    for g in range(n_kv):
        slot = w_wait(g, 'kv')
        kv_ref[chip, g] = product(h_ref, chip, slot).astype(BF16)
        nxt = g + DEPTH
        w_start(nxt, 'kv' if nxt < n_kv else 'q')
        kv_own(g, 'r').start()
        kv_own(g, 'l').start()

    def kv_in(c, g):
        return remote(kv_ref.at[c, g], kv_ref.at[c, g], kvf_sem.at[g], kvr_sem.at[c, g], lane(right))

    def kv_relay(g):
        kv_in(left, g).wait_recv()
        kv_in(right, g).wait_recv()
        if g < n_kv // 2:
            remote(kv_ref.at[left, g], kv_ref.at[left, g], kvf_sem.at[g], kvr_sem.at[left, g], lane(right)).start()
        else:
            remote(kv_ref.at[right, g], kv_ref.at[right, g], kvf_sem.at[g], kvr_sem.at[right, g], lane(left)).start()

    x_copy.wait_send()
    span = half // n_kv
    for part in range(n_kv):
        @pl.loop(0, span)
        def _(t):
            j = part * span + t
            slot = w_wait(n_kv + j, 'q')
            q_ref[j] = product(h_ref, chip, slot).astype(BF16)
            nxt = n_kv + j + DEPTH

            @pl.when(nxt < n_kv + half)
            def _():
                w_start(nxt, 'q')

            @pl.when(nxt >= n_kv + half)
            def _():
                w_start(nxt, 'o')
        kv_relay(part)

    def attend(g, r):
        n_h = 2 * per
        hb = n_h // 2
        m_rows = hb * rows

        def blk(c, start, size, diag):
            k_blk = kv_ref[c, g, start:start + size, :HEAD]
            v_blk = kv_ref[c, g, start:start + size, HEAD:]
            for u in range(2):
                q_u = jnp.concatenate([q_ref[g * per + (u * hb + i) // 2, r * rows:(r + 1) * rows, ((u * hb + i) % 2) * HEAD:((u * hb + i) % 2 + 1) * HEAD] for i in range(hb)], axis=0)
                s = lax.dot_general(q_u, k_blk, (((1,), (1,)), ((), ())), preferred_element_type=F32)
                if diag:
                    a = lax.broadcasted_iota(jnp.int32, (rows, size), 0) + r * rows
                    b = lax.broadcasted_iota(jnp.int32, (rows, size), 1)
                    s = s + jnp.concatenate([jnp.where(a >= b, 0.0, NEG)] * hb, axis=0)
                cols = [s[:, b * HEAD:(b + 1) * HEAD] for b in range(size // HEAD)]
                mx = functools.reduce(jnp.maximum, cols)
                mx = jnp.broadcast_to(jnp.max(mx, axis=1, keepdims=True), (m_rows, HEAD))
                if not diag:
                    m_old = m_ref[u]
                    mx = jnp.maximum(m_old, mx)
                ps = [jnp.exp2((y - mx) * LOG_SCALE) for y in cols]
                l = functools.reduce(jnp.add, ps)
                pv = jnp.dot(jnp.concatenate([p.astype(BF16) for p in ps], axis=1), v_blk, preferred_element_type=F32)
                if not diag:
                    a = jnp.exp2((m_old - mx) * LOG_SCALE)
                    l = l + l_ref[u] * a
                    pv = pv + acc_ref[u] * a
                m_ref[u] = mx
                l_ref[u] = l
                acc_ref[u] = pv

        blk(chip, 0, (r + 1) * rows, True)

        @pl.loop(0, chip)
        def _(c):
            blk(c, 0, 2 * rows, False)

        for u in range(2):
            o = (acc_ref[u] / jnp.sum(l_ref[u], axis=1, keepdims=True)).astype(BF16)
            for i in range(hb):
                h = u * hb + i
                o_ref[0, mine + g * per + h // 2, r * rows:(r + 1) * rows, (h % 2) * HEAD:(h % 2 + 1) * HEAD] = o[i * rows:(i + 1) * rows]

    def o_copy(g):
        part = o_ref.at[0, pl.ds(mine + g * per, per)]
        return remote(part, part, os_sem.at[g], or_sem.at[g], {'sp': sib})

    def o_in(g):
        part = o_ref.at[0, pl.ds(half - mine + g * per, per)]
        return remote(part, part, os_sem.at[g], or_sem.at[g], {'sp': sib})

    @pl.loop(0, n_kv)
    def _(g):
        @pl.when(g < n_kv // 2)
        def _():
            kv_in(opp, g).wait_recv()

        @pl.when(g >= n_kv // 2)
        def _():
            kv_in(opp, g).wait_recv()
        attend(g, 0)
        attend(g, 1)
        o_copy(g).start()

    for g in range(n_kv):
        o_in(g).wait_recv()

    def h_own(j, k, dev):
        ref = h_ref.at[chip, mine + j]
        return remote(ref, ref, hs_sem.at[k, j], hr_sem.at[chip, mine + j], dev)

    def h_own3(j):
        return (h_own(j, 0, lane(right)), h_own(j, 1, lane(left)), h_own(j, 2, {'sp': sib}))

    @pl.loop(0, half)
    def _(j):
        i = n_kv + half + j
        slot = w_wait(i, 'o')
        y = product(o_ref, 0, slot)
        h_ref[chip, mine + j] = (h_ref[chip, mine + j].astype(F32) + y).astype(BF16)

        @pl.when(i + DEPTH < n_w)
        def _():
            w_start(i + DEPTH, 'o')
        for cp in h_own3(j):
            cp.start()

    first = lax.rem(chip + 1, 2)
    second = first + 2
    base = (chip // 2) * (half // 2)

    def h_fwd(c, k, j):
        ref = h_ref.at[c, mine + j]
        return remote(ref, ref, hf_sem.at[k, j], hr_sem.at[c, mine + j], {'sp': sib})

    def h_relay(c, to, k, t):
        ref = h_ref.at[c, mine + base + t]
        return remote(ref, ref, hrel_sem.at[k, t], hr_sem.at[c, mine + base + t], lane(to))

    for k, (c, to) in enumerate(((first, second), (second, first))):
        @pl.loop(0, half)
        def _(j):
            h_fwd(c, k, j).wait_recv()
            t = j - base

            @pl.when((t >= 0) & (t < half // 2))
            def _():
                h_relay(c, to, k, t).start()
            h_fwd(c, k, j).start()

    @pl.loop(0, half)
    def _(j):
        h_fwd(opp, 2, j).wait_recv()
        h_fwd(opp, 2, j).start()

    def from_sib(c, j):
        ref = h_ref.at[c, half - mine + j]
        return remote(ref, ref, hs_sem.at[0, j], hr_sem.at[c, half - mine + j], {'sp': sib})

    @pl.loop(0, half)
    def _(j):
        for c in range(chips):
            from_sib(c, j).wait_recv()
        for cp in h_own3(j):
            cp.wait_send()
        for k, c in enumerate((first, second, opp)):
            h_fwd(c, k, j).wait_send()

    @pl.loop(0, half // 2)
    def _(t):
        h_relay(first, second, 0, t).wait_send()
        h_relay(second, first, 1, t).wait_send()
    for g in range(n_kv):
        kv_own(g, 'r').wait_send()
        kv_own(g, 'l').wait_send()
        kv_in(left, g).wait_send()
        o_copy(g).wait_send()
    tab_own.wait()
    for cp in tab_copies:
        cp.wait()


def route_kernel(tab_ref, h_ref, buf_ref, out_ref):
    me = lax.axis_index('sp')
    s = pl.program_id(0)
    c = s // 2
    rows = buf_ref.shape[0]
    experts = tab_ref.shape[1] - 8
    tab = tab_ref[s]
    ids = tab[:2].astype(jnp.int32)
    probs = tab[8:]
    exp_row = lax.broadcasted_iota(jnp.int32, (experts, rows), 0)
    hit = jnp.max(jnp.where(ids == me, 1.0, 0.0), axis=0, keepdims=True)
    both = jnp.where((exp_row == ids[0:1]) | (exp_row == ids[1:2]), probs, 0.0)
    p_me = jnp.sum(jnp.where(exp_row == me, probs, 0.0), axis=0, keepdims=True)
    gate = p_me * hit / jnp.sum(both, axis=0, keepdims=True)
    a = lax.broadcasted_iota(jnp.int32, (rows, rows), 0)
    b = lax.broadcasted_iota(jnp.int32, (rows, rows), 1)
    before = jnp.where(a < b, 1.0, 0.0).astype(BF16)
    slot = jnp.dot(jnp.broadcast_to(hit, (8, rows)).astype(BF16), before, preferred_element_type=F32)[:1].astype(jnp.int32)
    pick = (a == slot) & (hit > 0.5)
    g_slot = jnp.sum(jnp.where(pick, gate, 0.0), axis=1, keepdims=True)
    pick = jnp.where(pick, 1.0, 0.0).astype(BF16)
    lo = pl.ds(pl.multiple_of(lax.rem(s, 2) * rows, rows), rows)
    own = s == me
    for j in range(h_ref.shape[1]):
        got = jnp.dot(pick, h_ref[c, j, lo], preferred_element_type=F32)
        buf_ref[:, j * CW:(j + 1) * CW] = (g_slot * got).astype(BF16)

    @pl.when(s == me)
    def _():
        for j in range(h_ref.shape[1]):
            out_ref[:, j * CW:(j + 1) * CW] = h_ref[c, j, lo]


def solution(mesh):
    group = mesh.shape['sp']
    row_spec = P(('dp', 'sp'), None)
    buf_spec = P(('dp', 'sp'), None, None)

    def step(x, w_q, w_k, w_v, w_o, ids, probs):
        rows, width = x.shape
        experts = probs.shape[1]
        chips = group // 2
        n_col = width // CW
        half = n_col // 2
        n_kv = w_k.shape[1] // HEAD // 2
        per = half // n_kv
        crow = 2 * rows
        tab = jnp.concatenate([ids.T.astype(F32), jnp.zeros((6, rows), F32), probs.T], axis=0)
        dma = pltpu.SemaphoreType.DMA
        hbm = pl.BlockSpec(memory_space=pl.ANY)
        vm = pl.BlockSpec(memory_space=pltpu.VMEM)
        h_all, tabs = pl.pallas_call(
            functools.partial(block_kernel, group),
            in_specs=[hbm] * 5 + [vm],
            out_specs=[vm, vm],
            out_shape=[
                pltpu.VMEM((chips, n_col, crow, CW), BF16),
                pltpu.VMEM((group, tab.shape[0], rows), F32),
            ],
            scratch_shapes=[
                pltpu.VMEM((half, crow, CW), BF16),
                pltpu.VMEM((1, n_col, crow, CW), BF16),
                pltpu.VMEM((chips, n_kv, crow, CW), BF16),
                pltpu.VMEM((DEPTH, width, CW), BF16),
                pltpu.VMEM((2, per * rows, HEAD), F32),
                pltpu.VMEM((2, per * rows, HEAD), F32),
                pltpu.VMEM((2, per * rows, HEAD), F32),
                dma((DEPTH, 2)), dma((n_col,)), dma, dma,
                dma((2, n_kv)), dma((chips, n_kv)), dma((n_kv,)), dma((n_kv,)), dma((n_kv,)),
                dma((3, half)), dma((3, half)), dma((2, half // 2)), dma((chips, n_col)),
                dma((group,)), dma((group,)),
            ],
            compiler_params=pltpu.CompilerParams(collective_id=0, has_side_effects=True, vmem_limit_bytes=38 * 1024 * 1024),
        )(x, w_q, w_k, w_v, w_o, tab)
        buf, hidden_out = pl.pallas_call(
            route_kernel,
            grid=(group,),
            in_specs=[vm, vm],
            out_specs=[pl.BlockSpec((rows, width), lambda s: (s, 0)), pl.BlockSpec((rows, width), lambda s: (0, 0))],
            out_shape=[jax.ShapeDtypeStruct((group * rows, width), BF16), jax.ShapeDtypeStruct((rows, width), BF16)],
            compiler_params=pltpu.CompilerParams(vmem_limit_bytes=24 * 1024 * 1024),
        )(pltpu.with_memory_space_constraint(tabs, pltpu.VMEM), pltpu.with_memory_space_constraint(h_all, pltpu.VMEM))
        return hidden_out, buf[None]

    return jax.shard_map(step, mesh=mesh, in_specs=(row_spec, P(), P(), P(), P(), row_spec, row_spec), out_specs=(row_spec, buf_spec), check_vma=False)
```

time: 805 us -> 238 us (0.30)
  blocking collectives: 280 us -> 0 us
  Pallas kernels: 0 us -> 218 us
  local copies, waits for them, and re-layouts: 232 us -> 17.1 us
  matrix products: 158 us -> 0 us
  waiting for transfers between devices: 62 us -> 0 us
  other arithmetic: 48.6 us -> 2.06 us
  starting transfers between devices: 20.6 us -> 0 us
    all_to_all x1 -> x0, blocking collectives: 280 us -> none  [device_step(): recv_buf = lax.all_to_all(send_buf, 'sp', 0, 1, tiled=True)]
    pallas_call x0 -> x2, Pallas kernels: none -> 218 us  [the longest x1 204 us: step(): pl.pallas_call(functools.partial(block_kernel, group), in_specs=[hbm] * 5...]
    scatter x1 -> x0, local copies, waits for them, and re-layouts: 175 us -> none  [route_rows(): return send_buf.at[expert_ids, slot_rank].set(gated, unique_indices=True)]
    dot_general x6 -> x0, matrix products: 158 us -> none  [the longest x1 40.7 us: device_step(): jnp.einsum('gmqk,kgd->qgmd', weights, v_seq, preferred_element_type=jnp.f...]
    all_to_all x4 -> x0, waiting for transfers between devices: 62 us -> none  [the longest x1 38.9 us: device_step(): lax.all_to_all(attn_seq, 'sp', 0, 1, tiled=True)]
    reduce_sum x3 -> x0, other arithmetic: 35.2 us -> none  [the longest x1 35.2 us: device_step(): jax.nn.softmax(jnp.where(causal, scores, -1e+30), axis=-1)]
    all_to_all x4 -> x0, starting transfers between devices: 20.6 us -> none  [the longest x1 6.01 us: device_step(): q_seq = lax.all_to_all(q_loc, 'sp', 1, 0, tiled=True)]
    convert_element_type x1 -> x0, local copies, waits for them, and re-layouts: 13.3 us -> none  [route_rows(): (gate_w[:, :, None] * hidden_out[:, None, :].astype(jnp.float32)).astype(...]
  transfers between devices with their start and end apart: 4 -> 0, of which waited for: 3 -> 0; matrix products, arithmetic and copies ran while one was open for 13% -> 0% of each run, Pallas kernels for 0% -> 0%
where the time goes in v2:
time: 238 us
  Pallas kernels  218 us (92%)
  local copies, waits for them, and re-layouts  17.1 us (7%)
    pallas_call x1, Pallas kernels, step(): pl.pallas_call(functools.partial(block_kernel, group), in_specs=[hbm] * 5...  204 us
    unnamed x4, local copies, waits for them, and re-layouts  17.1 us
    pallas_call x1, Pallas kernels, step(): pl.pallas_call(route_kernel, grid=(group,), in_specs=[vm, vm], out_specs=...  13.6 us

profile of v2, /device:TPU:113, one launch (start us, length us, event | category | flops | bytes accessed | tf_op | source)
XLA Modules:
  0.0 237.9 jit_solution(119529252250760409)
XLA Ops:
  0.6 0.1 pad.1.clone
  0.7 0.7 convert_bitcast_fusion
  1.4 1.4 pad_maximum_fusion.tab_ref
  2.8 204.4 %shard_map.86 = (bf16[4,24,512,256]{3,2,1,0:T(8,128)(2,1)S(1)}, f32[8,16,256]{2,1,0:T(8,128)S(1)}) custom-call(bf16[256,6144]{1,0:T(8,128)(2,1)} %x_ref.1, bf16[6144,6144]{1,0:T(8,128)(2,1)} %wq_ref.1, bf16[6144,1024]{1,0:T(8,128)(2,1)} %wk_ref.1, bf16[6144,1024]{1,0:T(8,128)(2,1)} %wv_ref.1, bf16[6144,6144]{1,0:T(8,128)(2,1)} %wo_ref.1, ...), custom_call_target="tpu_custom_call" | custom-call | tf_op jit(solution)/shard_map/pallas_call | solution.py:331
  207.2 0.0 copy-start
  207.2 8.9 %copy-done = bf16[4,24,512,256]{3,2,1,0:T(8,128)(2,1)} copy-done((bf16[4,24,512,256]{3,2,1,0:T(8,128)(2,1)}, bf16[4,24,512,256]{3,2,1,0:T(8,128)(2,1)S(1)}, u32[]{:S(2)}) %copy-start) | copy-done | bytes 25165848
  216.1 0.0 copy-start.1
  216.1 8.2 %copy-done.1 = bf16[4,24,512,256]{3,2,1,0:T(8,128)(2,1)S(1)} copy-done((bf16[4,24,512,256]{3,2,1,0:T(8,128)(2,1)S(1)}, bf16[4,24,512,256]{3,2,1,0:T(8,128)(2,1)}, u32[]{:S(2)}) %copy-start.1) | copy-done | bytes 25165848
  224.3 13.6 %shard_map.87 = (bf16[2048,6144]{1,0:T(8,128)(2,1)}, bf16[256,6144]{1,0:T(8,128)(2,1)}) custom-call(f32[8,16,256]{2,1,0:T(8,128)S(1)} %get-tuple-element.6.tab_ref, bf16[4,24,512,256]{3,2,1,0:T(8,128)(2,1)S(1)} %copy-done.1), custom_call_target="tpu_custom_call" | custom-call | tf_op jit(solution)/shard_map/pallas_call | solution.py:354
  (1 shorter events, 0.0 us)
Async XLA Ops:
  207.2 8.9 %copy-start = (bf16[4,24,512,256]{3,2,1,0:T(8,128)(2,1)}, bf16[4,24,512,256]{3,2,1,0:T(8,128)(2,1)S(1)}, u32[]{:S(2)}) copy-start(bf16[4,24,512,256]{3,2,1,0:T(8,128)(2,1)S(1)} %get-tuple-element.7.h_ref) | copy-start | bytes 75497472
  216.1 8.2 %copy-start.1 = (bf16[4,24,512,256]{3,2,1,0:T(8,128)(2,1)S(1)}, bf16[4,24,512,256]{3,2,1,0:T(8,128)(2,1)}, u32[]{:S(2)}) copy-start(bf16[4,24,512,256]{3,2,1,0:T(8,128)(2,1)} %copy-done) | copy-start | bytes 75497472

commit v3 on v2

v3 whole, which is shorter than its diff:
```python
import functools
import math
import jax
import jax.numpy as jnp
from jax import lax
from jax.experimental import pallas as pl
from jax.experimental.pallas import tpu as pltpu
from jax.sharding import PartitionSpec as P

HEAD = 128
LOG_SCALE = math.log2(math.e) / math.sqrt(HEAD)
NEG = -1e30
CW = 2 * HEAD
DEPTH = 4
SHARE = 7
BF16 = jnp.bfloat16
F32 = jnp.float32
MESH = pl.DeviceIdType.MESH


def block_kernel(group, x_ref, wq_ref, wk_ref, wv_ref, wo_ref, tab_ref, h_ref, tabs_ref,
                 xs_ref, q_ref, o_ref, kv_ref, w_ref, hs_ref, m_ref, l_ref, acc_ref,
                 w_sem, x_sem, xs_sem, xr_sem, kvs_sem, kvr_sem, kvf_sem, os_sem, or_sem,
                 hs_sem, hf_sem, hrel_sem, hr_sem, ts_sem, tr_sem):
    me = lax.axis_index('sp')
    chips = group // 2
    chip, core = me // 2, lax.rem(me, 2)
    rows = x_ref.shape[0]
    n_col = x_ref.shape[1] // CW
    half = n_col // 2
    n_kv = wk_ref.shape[1] // HEAD // 2
    per = half // n_kv
    mine = core * half
    sib = chip * 2 + (1 - core)
    right = lax.rem(chip + 1, chips)
    left = lax.rem(chip + chips - 1, chips)
    opp = lax.rem(chip + 2, chips)

    def lane(c):
        return {'sp': c * 2 + core}

    def remote(src, dst, send, recv, dev):
        return pltpu.make_async_remote_copy(src_ref=src, dst_ref=dst, send_sem=send, recv_sem=recv, device_id=dev, device_id_type=MESH)

    n_w = n_kv + 4 * half

    def w_start(i, stage):
        slot = lax.rem(i, DEPTH)
        if stage == 'kv':
            col = pl.multiple_of((core * n_kv + i) * HEAD, HEAD)
            pltpu.make_async_copy(wk_ref.at[:, pl.ds(col, HEAD)], w_ref.at[slot, :, pl.ds(0, HEAD)], w_sem.at[slot, 0]).start()
            pltpu.make_async_copy(wv_ref.at[:, pl.ds(col, HEAD)], w_ref.at[slot, :, pl.ds(HEAD, HEAD)], w_sem.at[slot, 1]).start()
        else:
            src = wq_ref if stage == 'q' else wo_ref
            j = lax.rem(i - n_kv, half)
            col = pl.multiple_of((mine + j) * CW, CW)
            pltpu.make_async_copy(src.at[:, pl.ds(col, CW)], w_ref.at[slot], w_sem.at[slot, 0]).start()

    def w_wait(i, stage):
        slot = lax.rem(i, DEPTH)
        if stage == 'kv':
            pltpu.make_async_copy(wk_ref.at[:, pl.ds(0, HEAD)], w_ref.at[slot, :, pl.ds(0, HEAD)], w_sem.at[slot, 0]).wait()
            pltpu.make_async_copy(wv_ref.at[:, pl.ds(0, HEAD)], w_ref.at[slot, :, pl.ds(HEAD, HEAD)], w_sem.at[slot, 1]).wait()
        else:
            pltpu.make_async_copy(wq_ref.at[:, pl.ds(0, CW)], w_ref.at[slot], w_sem.at[slot, 0]).wait()
        return slot

    own_rows = pl.ds(pl.multiple_of(core * rows, rows), rows)
    for j in range(n_col):
        pltpu.make_async_copy(x_ref.at[:, pl.ds(j * CW, CW)], xs_ref.at[j, own_rows], x_sem.at[j]).start()
    for i in range(DEPTH):
        w_start(i, 'kv' if i < n_kv else 'q')

    barrier = pltpu.get_barrier_semaphore()
    for d in range(1, group):
        pl.semaphore_signal(barrier, inc=1, device_id={'sp': lax.rem(me + d, group)}, device_id_type=MESH)
    pl.semaphore_wait(barrier, group - 1)

    for j in range(n_col):
        pltpu.make_async_copy(x_ref.at[:, pl.ds(j * CW, CW)], xs_ref.at[j, own_rows], x_sem.at[j]).wait()
    x_copy = remote(xs_ref.at[:, own_rows], xs_ref.at[:, own_rows], xs_sem, xr_sem, {'sp': sib})
    x_copy.start()
    tab_own = pltpu.make_async_copy(tab_ref, tabs_ref.at[me], ts_sem.at[0])
    tab_own.start()
    tab_copies = []
    for d in range(1, group):
        cp = remote(tab_ref, tabs_ref.at[me], ts_sem.at[d], tr_sem.at[d], {'sp': lax.rem(me + d, group)})
        cp.start()
        tab_copies.append(cp)
    x_copy.wait_recv()

    def product(lhs_ref, slot):
        lhs = jnp.concatenate([lhs_ref[j] for j in range(n_col)], axis=1)
        return jnp.dot(lhs, w_ref[slot], preferred_element_type=F32)

    def kv_own(g, to):
        s = 0 if to == 'r' else 1
        return remote(kv_ref.at[chip, g], kv_ref.at[chip, g], kvs_sem.at[s, g], kvr_sem.at[chip, g], lane(right if to == 'r' else left))

    for g in range(n_kv):
        slot = w_wait(g, 'kv')
        kv_ref[chip, g] = product(xs_ref, slot).astype(BF16)
        nxt = g + DEPTH
        w_start(nxt, 'kv' if nxt < n_kv else 'q')
        kv_own(g, 'r').start()
        kv_own(g, 'l').start()

    def kv_in(c, g):
        return remote(kv_ref.at[c, g], kv_ref.at[c, g], kvf_sem.at[g], kvr_sem.at[c, g], lane(right))

    def kv_relay(g):
        kv_in(left, g).wait_recv()
        kv_in(right, g).wait_recv()
        if g < n_kv // 2:
            remote(kv_ref.at[left, g], kv_ref.at[left, g], kvf_sem.at[g], kvr_sem.at[left, g], lane(right)).start()
        else:
            remote(kv_ref.at[right, g], kv_ref.at[right, g], kvf_sem.at[g], kvr_sem.at[right, g], lane(left)).start()

    def w_next(i):
        nxt = i + DEPTH
        lap = (nxt - n_kv) // half

        @pl.when((nxt < n_w) & (lax.rem(lap, 2) == 0))
        def _():
            w_start(nxt, 'q')

        @pl.when((nxt < n_w) & (lax.rem(lap, 2) == 1))
        def _():
            w_start(nxt, 'o')

    def queries(r, lo, n):
        @pl.loop(lo, lo + n)
        def _(j):
            i = n_kv + 2 * r * half + j
            slot = w_wait(i, 'q')
            q_ref[j] = product(xs_ref.at[:, r * rows:(r + 1) * rows], slot).astype(BF16)
            w_next(i)

    span = half // n_kv
    for part in range(n_kv):
        queries(0, part * span, span)
        if part < n_kv - 1:
            kv_relay(part)

    n_h = 2 * per
    hb = n_h // 2
    m_rows = hb * rows

    def blk(g, r, c, size, diag):
        k_blk = kv_ref[c, g, :size, :HEAD]
        v_blk = kv_ref[c, g, :size, HEAD:]
        scores = []
        for u in range(2):
            q_u = jnp.concatenate([q_ref[g * per + (u * hb + i) // 2, :, ((u * hb + i) % 2) * HEAD:((u * hb + i) % 2 + 1) * HEAD] for i in range(hb)], axis=0)
            scores.append(lax.dot_general(q_u, k_blk, (((1,), (1,)), ((), ())), preferred_element_type=F32))
        for u in range(2):
            s = scores[u]
            if diag:
                a = lax.broadcasted_iota(jnp.int32, (rows, size), 0) + r * rows
                b = lax.broadcasted_iota(jnp.int32, (rows, size), 1)
                s = s + jnp.concatenate([jnp.where(a >= b, 0.0, NEG)] * hb, axis=0)
            cols = [s[:, b * HEAD:(b + 1) * HEAD] for b in range(size // HEAD)]
            mx = functools.reduce(jnp.maximum, cols)
            mx = jnp.broadcast_to(jnp.max(mx, axis=1, keepdims=True), (m_rows, HEAD))
            if not diag:
                m_old = m_ref[g, u]
                mx = jnp.maximum(m_old, mx)
            ps = [jnp.exp2((y - mx) * LOG_SCALE) for y in cols]
            l = functools.reduce(jnp.add, ps)
            pv = jnp.dot(jnp.concatenate([p.astype(BF16) for p in ps], axis=1), v_blk, preferred_element_type=F32)
            if not diag:
                a = jnp.exp2((m_old - mx) * LOG_SCALE)
                l = l + l_ref[g, u] * a
                pv = pv + acc_ref[g, u] * a
            m_ref[g, u] = mx
            l_ref[g, u] = l
            acc_ref[g, u] = pv

    def finish(g, r):
        for u in range(2):
            o = (acc_ref[g, u] / jnp.sum(l_ref[g, u], axis=1, keepdims=True)).astype(BF16)
            for i in range(hb):
                h = u * hb + i
                o_ref[r, mine + g * per + h // 2, :, (h % 2) * HEAD:(h % 2 + 1) * HEAD] = o[i * rows:(i + 1) * rows]

    def o_copy(r, g):
        part = o_ref.at[r, pl.ds(mine + g * per, per)]
        return remote(part, part, os_sem.at[r, g], or_sem.at[r, g], {'sp': sib})

    def o_in(r, g):
        part = o_ref.at[r, pl.ds(half - mine + g * per, per)]
        return remote(part, part, os_sem.at[r, g], or_sem.at[r, g], {'sp': sib})

    def piece(s, j):
        return h_ref.at[pl.ds(pl.multiple_of(s * rows, rows), rows), pl.ds(pl.multiple_of(j * CW, CW), CW)]

    def h_own(r, j, k, dev):
        s = chip * 2 + r
        return remote(hs_ref.at[r, j], piece(s, mine + j), hs_sem.at[k, r, j], hr_sem.at[s, mine + j], dev)

    def h_own3(r, j):
        return (h_own(r, j, 0, lane(right)), h_own(r, j, 1, lane(left)), h_own(r, j, 2, {'sp': sib}))

    def h_keep(r, j):
        return pltpu.make_async_copy(hs_ref.at[r, j], piece(chip * 2 + r, mine + j), hs_sem.at[3, r, j])

    def project(r):
        @pl.loop(0, half)
        def _(j):
            i = n_kv + (1 + 2 * r) * half + j
            slot = w_wait(i, 'o')
            y = product(o_ref.at[r], slot)
            hs_ref[r, j] = (xs_ref[mine + j, r * rows:(r + 1) * rows].astype(F32) + y).astype(BF16)

            w_next(i)
            for cp in h_own3(r, j):
                cp.start()
            h_keep(r, j).start()

    first = lax.rem(chip + 1, 2)
    second = first + 2
    early = chip < chips // 2

    def h_fwd(c, r, k, j):
        ref = piece(c * 2 + r, mine + j)
        return remote(ref, ref, hf_sem.at[k, r, j], hr_sem.at[c * 2 + r, mine + j], {'sp': sib})

    def h_relay(c, to, r, k, j):
        ref = piece(c * 2 + r, mine + j)
        return remote(ref, ref, hrel_sem.at[k, r, j], hr_sem.at[c * 2 + r, mine + j], lane(to))

    cut = half * SHARE // 12

    def relayed(j):
        return early == (j < cut)

    def relay(k, r):
        c, to = ((first, second), (second, first))[k]

        @pl.loop(0, half)
        def _(j):
            h_fwd(c, r, k, j).wait_recv()

            @pl.when(relayed(j))
            def _():
                h_relay(c, to, r, k, j).start()
            h_fwd(c, r, k, j).start()

    late, last = chip >= chips // 2, chip == chips - 1
    for r in range(2):
        if r == 1:
            queries(1, 0, half)

        @pl.loop(0, n_kv)
        def _(g):
            if r == 0:
                pl.when(g == 1)(lambda: kv_relay(n_kv - 1))
            else:
                pl.when((g == 1) & late)(lambda: relay(0, 0))
                pl.when((g == 2) & last)(lambda: relay(1, 0))
            blk(g, r, chip, (r + 1) * rows, True)

            @pl.loop(0, 2)
            def _(n):
                c = n * right + (1 - n) * left

                @pl.when(c < chip)
                def _():
                    blk(g, r, c, 2 * rows, False)

        @pl.loop(0, n_kv)
        def _(g):
            if r == 0:
                kv_in(opp, g).wait_recv()

            @pl.when(opp < chip)
            def _():
                blk(g, r, opp, 2 * rows, False)
            finish(g, r)
            o_copy(r, g).start()
        for g in range(n_kv):
            o_in(r, g).wait_recv()
        project(r)

    pl.when(jnp.logical_not(late))(lambda: relay(0, 0))
    pl.when(jnp.logical_not(last))(lambda: relay(1, 0))
    relay(0, 1)
    relay(1, 1)
    for r in range(2):
        @pl.loop(0, half)
        def _(j):
            h_fwd(opp, r, 2, j).wait_recv()
            h_fwd(opp, r, 2, j).start()

    def from_sib(c, r, j):
        ref = piece(c * 2 + r, half - mine + j)
        return remote(ref, ref, hs_sem.at[0, r, j], hr_sem.at[c * 2 + r, half - mine + j], {'sp': sib})

    for r in range(2):
        @pl.loop(0, half)
        def _(j):
            for c in range(chips):
                from_sib(c, r, j).wait_recv()
            for cp in h_own3(r, j):
                cp.wait_send()
            h_keep(r, j).wait()
            for k, c in enumerate((first, second, opp)):
                h_fwd(c, r, k, j).wait_send()

            @pl.when(relayed(j))
            def _():
                h_relay(first, second, r, 0, j).wait_send()
                h_relay(second, first, r, 1, j).wait_send()
    for g in range(n_kv):
        kv_own(g, 'r').wait_send()
        kv_own(g, 'l').wait_send()
        kv_in(left, g).wait_send()
        for r in range(2):
            o_copy(r, g).wait_send()
    x_copy.wait_send()
    tab_own.wait()
    for cp in tab_copies:
        cp.wait()


def route_kernel(tab_ref, h_ref, buf_ref, out_ref):
    me = lax.axis_index('sp')
    s = pl.program_id(0)
    rows = buf_ref.shape[0]
    experts = tab_ref.shape[1] - 8
    tab = tab_ref[0]
    ids = tab[:2].astype(jnp.int32)
    probs = tab[8:]
    exp_row = lax.broadcasted_iota(jnp.int32, (experts, rows), 0)
    hit = jnp.max(jnp.where(ids == me, 1.0, 0.0), axis=0, keepdims=True)
    both = jnp.where((exp_row == ids[0:1]) | (exp_row == ids[1:2]), probs, 0.0)
    p_me = jnp.sum(jnp.where(exp_row == me, probs, 0.0), axis=0, keepdims=True)
    gate = p_me * hit / jnp.sum(both, axis=0, keepdims=True)
    a = lax.broadcasted_iota(jnp.int32, (rows, rows), 0)
    b = lax.broadcasted_iota(jnp.int32, (rows, rows), 1)
    before = jnp.where(a < b, 1.0, 0.0).astype(BF16)
    slot = jnp.dot(jnp.broadcast_to(hit, (8, rows)).astype(BF16), before, preferred_element_type=F32)[:1].astype(jnp.int32)
    pick = (a == slot) & (hit > 0.5)
    g_slot = jnp.sum(jnp.where(pick, gate, 0.0), axis=1, keepdims=True)
    pick = jnp.where(pick, 1.0, 0.0).astype(BF16)
    for j in range(buf_ref.shape[1] // CW):
        cols = slice(j * CW, (j + 1) * CW)
        got = jnp.dot(pick, h_ref[:, cols], preferred_element_type=F32)
        buf_ref[:, cols] = (g_slot * got).astype(BF16)

    @pl.when(s == me)
    def _():
        out_ref[...] = h_ref[...]


def solution(mesh):
    group = mesh.shape['sp']
    row_spec = P(('dp', 'sp'), None)
    buf_spec = P(('dp', 'sp'), None, None)

    def step(x, w_q, w_k, w_v, w_o, ids, probs):
        rows, width = x.shape
        experts = probs.shape[1]
        chips = group // 2
        n_col = width // CW
        half = n_col // 2
        n_kv = w_k.shape[1] // HEAD // 2
        per = half // n_kv
        crow = 2 * rows
        tab = jnp.concatenate([ids.T.astype(F32), jnp.zeros((6, rows), F32), probs.T], axis=0)
        dma = pltpu.SemaphoreType.DMA
        hbm = pl.BlockSpec(memory_space=pl.ANY)
        vm = pl.BlockSpec(memory_space=pltpu.VMEM)
        h_all, tabs = pl.pallas_call(
            functools.partial(block_kernel, group),
            in_specs=[hbm] * 5 + [vm],
            out_specs=[hbm, hbm],
            out_shape=[
                jax.ShapeDtypeStruct((group * rows, width), BF16),
                jax.ShapeDtypeStruct((group, tab.shape[0], rows), F32),
            ],
            scratch_shapes=[
                pltpu.VMEM((n_col, crow, CW), BF16),
                pltpu.VMEM((half, rows, CW), BF16),
                pltpu.VMEM((2, n_col, rows, CW), BF16),
                pltpu.VMEM((chips, n_kv, crow, CW), BF16),
                pltpu.VMEM((DEPTH, width, CW), BF16),
                pltpu.VMEM((2, half, rows, CW), BF16),
                pltpu.VMEM((n_kv, 2, per * rows, HEAD), F32),
                pltpu.VMEM((n_kv, 2, per * rows, HEAD), F32),
                pltpu.VMEM((n_kv, 2, per * rows, HEAD), F32),
                dma((DEPTH, 2)), dma((n_col,)), dma, dma,
                dma((2, n_kv)), dma((chips, n_kv)), dma((n_kv,)), dma((2, n_kv)), dma((2, n_kv)),
                dma((4, 2, half)), dma((3, 2, half)), dma((2, 2, half)), dma((group, n_col)),
                dma((group,)), dma((group,)),
            ],
            compiler_params=pltpu.CompilerParams(collective_id=0, has_side_effects=True, vmem_limit_bytes=56 * 1024 * 1024),
        )(x, w_q, w_k, w_v, w_o, tab)
        buf, hidden_out = pl.pallas_call(
            route_kernel,
            grid=(group,),
            in_specs=[pl.BlockSpec((1, tab.shape[0], rows), lambda s: (s, 0, 0)), pl.BlockSpec((rows, width), lambda s: (s, 0))],
            out_specs=[pl.BlockSpec((rows, width), lambda s: (s, 0)), pl.BlockSpec((rows, width), lambda s: (0, 0))],
            out_shape=[jax.ShapeDtypeStruct((group * rows, width), BF16), jax.ShapeDtypeStruct((rows, width), BF16)],
        )(tabs, h_all)
        return hidden_out, buf[None]

    return jax.shard_map(step, mesh=mesh, in_specs=(row_spec, P(), P(), P(), P(), row_spec, row_spec), out_specs=(row_spec, buf_spec), check_vma=False)
```

time: 238 us -> 203 us (0.85)
  Pallas kernels: 218 us -> 199 us
  local copies, waits for them, and re-layouts: 17.1 us -> 0.08 us
    pallas_call x1, Pallas kernels: 204 us -> 176 us  [step(): pl.pallas_call(functools.partial(block_kernel, group), in_specs=[hbm] * 5...]
    unnamed x4 -> x0, local copies, waits for them, and re-layouts: 17.1 us -> none
    pallas_call x1, Pallas kernels: 13.6 us -> 22.9 us  [step(): pl.pallas_call(route_kernel, grid=(group,), in_specs=[pl.BlockSpec((1, ta...]
where the time goes in v3:
time: 203 us; the launch traced here: 202 us
  Pallas kernels  199 us (98%)
  other arithmetic  2.06 us (1%)
    pallas_call x1, Pallas kernels, step(): pl.pallas_call(functools.partial(block_kernel, group), in_specs=[hbm] * 5...  176 us
    pallas_call x1, Pallas kernels, step(): pl.pallas_call(route_kernel, grid=(group,), in_specs=[pl.BlockSpec((1, ta...  22.9 us

profile of v3, /device:TPU:113, one launch (start us, length us, event | category | flops | bytes accessed | tf_op | source)
XLA Modules:
  0.0 201.8 jit_solution(16758580167509186871)
XLA Ops:
  0.6 0.1 pad.1.clone
  0.7 0.7 convert_bitcast_fusion
  1.4 1.4 pad_maximum_fusion.tab_ref
  2.8 176.1 %shard_map.86 = (bf16[2048,6144]{1,0:T(8,128)(2,1)}, f32[8,16,256]{2,1,0:T(8,128)}) custom-call(bf16[256,6144]{1,0:T(8,128)(2,1)} %x_ref.1, bf16[6144,6144]{1,0:T(8,128)(2,1)} %wq_ref.1, bf16[6144,1024]{1,0:T(8,128)(2,1)} %wk_ref.1, bf16[6144,1024]{1,0:T(8,128)(2,1)} %wv_ref.1, bf16[6144,6144]{1,0:T(8,128)(2,1)} %wo_ref.1, f32[16,256]{1,0:T(8,128)} %pad_maximum_fusion.tab_ref), custom_call_target="tpu_custom_call" | custom-call | tf_op jit(solution)/shard_map/pallas_call | solution.py:374
  178.9 22.9 %shard_map.87 = (bf16[2048,6144]{1,0:T(8,128)(2,1)}, bf16[256,6144]{1,0:T(8,128)(2,1)}) custom-call(f32[8,16,256]{2,1,0:T(8,128)} %get-tuple-element.6.tab_ref, bf16[2048,6144]{1,0:T(8,128)(2,1)} %get-tuple-element.7.h_ref), custom_call_target="tpu_custom_call" | custom-call | tf_op jit(solution)/shard_map/pallas_call | solution.py:399
  (1 shorter events, 0.0 us)

commit v4 on v3

--- a/solution.py
+++ b/solution.py
@@ -13,13 +13,15 @@
 CW = 2 * HEAD
 DEPTH = 4
 SHARE = 7
+AHEAD = 4
+SLOTS = 4
 BF16 = jnp.bfloat16
 F32 = jnp.float32
 MESH = pl.DeviceIdType.MESH
 
 
 def block_kernel(group, x_ref, wq_ref, wk_ref, wv_ref, wo_ref, tab_ref, h_ref, tabs_ref,
-                 xs_ref, q_ref, o_ref, kv_ref, w_ref, hs_ref, m_ref, l_ref, acc_ref,
+                 xs_ref, q_ref, o_ref, ks_ref, kv_ref, w_ref, hs_ref, m_ref, l_ref, acc_ref,
                  w_sem, x_sem, xs_sem, xr_sem, kvs_sem, kvr_sem, kvf_sem, os_sem, or_sem,
                  hs_sem, hf_sem, hrel_sem, hr_sem, ts_sem, tr_sem):
     me = lax.axis_index('sp')
@@ -42,22 +44,23 @@
     def remote(src, dst, send, recv, dev):
         return pltpu.make_async_remote_copy(src_ref=src, dst_ref=dst, send_sem=send, recv_sem=recv, device_id=dev, device_id_type=MESH)
 
-    n_w = n_kv + 4 * half
+    n_k = 2 * n_kv
+    n_w = n_k + 4 * half
 
     def w_start(i, stage):
-        slot = lax.rem(i, DEPTH)
+        slot = lax.rem(jnp.int32(i), DEPTH)
         if stage == 'kv':
-            col = pl.multiple_of((core * n_kv + i) * HEAD, HEAD)
+            col = (i % 2 * n_kv + i // 2) * HEAD
             pltpu.make_async_copy(wk_ref.at[:, pl.ds(col, HEAD)], w_ref.at[slot, :, pl.ds(0, HEAD)], w_sem.at[slot, 0]).start()
             pltpu.make_async_copy(wv_ref.at[:, pl.ds(col, HEAD)], w_ref.at[slot, :, pl.ds(HEAD, HEAD)], w_sem.at[slot, 1]).start()
         else:
             src = wq_ref if stage == 'q' else wo_ref
-            j = lax.rem(i - n_kv, half)
+            j = lax.rem(i - n_k, half)
             col = pl.multiple_of((mine + j) * CW, CW)
             pltpu.make_async_copy(src.at[:, pl.ds(col, CW)], w_ref.at[slot], w_sem.at[slot, 0]).start()
 
     def w_wait(i, stage):
-        slot = lax.rem(i, DEPTH)
+        slot = lax.rem(jnp.int32(i), DEPTH)
         if stage == 'kv':
             pltpu.make_async_copy(wk_ref.at[:, pl.ds(0, HEAD)], w_ref.at[slot, :, pl.ds(0, HEAD)], w_sem.at[slot, 0]).wait()
             pltpu.make_async_copy(wv_ref.at[:, pl.ds(0, HEAD)], w_ref.at[slot, :, pl.ds(HEAD, HEAD)], w_sem.at[slot, 1]).wait()
@@ -69,56 +72,68 @@
     for j in range(n_col):
         pltpu.make_async_copy(x_ref.at[:, pl.ds(j * CW, CW)], xs_ref.at[j, own_rows], x_sem.at[j]).start()
     for i in range(DEPTH):
-        w_start(i, 'kv' if i < n_kv else 'q')
+        w_start(i, 'kv' if i < n_k else 'q')
 
     barrier = pltpu.get_barrier_semaphore()
     for d in range(1, group):
         pl.semaphore_signal(barrier, inc=1, device_id={'sp': lax.rem(me + d, group)}, device_id_type=MESH)
-    pl.semaphore_wait(barrier, group - 1)
 
     for j in range(n_col):
         pltpu.make_async_copy(x_ref.at[:, pl.ds(j * CW, CW)], xs_ref.at[j, own_rows], x_sem.at[j]).wait()
     x_copy = remote(xs_ref.at[:, own_rows], xs_ref.at[:, own_rows], xs_sem, xr_sem, {'sp': sib})
-    x_copy.start()
     tab_own = pltpu.make_async_copy(tab_ref, tabs_ref.at[me], ts_sem.at[0])
-    tab_own.start()
-    tab_copies = []
-    for d in range(1, group):
-        cp = remote(tab_ref, tabs_ref.at[me], ts_sem.at[d], tr_sem.at[d], {'sp': lax.rem(me + d, group)})
-        cp.start()
-        tab_copies.append(cp)
-    x_copy.wait_recv()
+    tab_copies = [remote(tab_ref, tabs_ref.at[me], ts_sem.at[d], tr_sem.at[d], {'sp': lax.rem(me + d, group)}) for d in range(1, group)]
 
     def product(lhs_ref, slot):
         lhs = jnp.concatenate([lhs_ref[j] for j in range(n_col)], axis=1)
         return jnp.dot(lhs, w_ref[slot], preferred_element_type=F32)
 
-    def kv_own(g, to):
-        s = 0 if to == 'r' else 1
-        return remote(kv_ref.at[chip, g], kv_ref.at[chip, g], kvs_sem.at[s, g], kvr_sem.at[chip, g], lane(right if to == 'r' else left))
-
-    for g in range(n_kv):
-        slot = w_wait(g, 'kv')
-        kv_ref[chip, g] = product(xs_ref, slot).astype(BF16)
-        nxt = g + DEPTH
-        w_start(nxt, 'kv' if nxt < n_kv else 'q')
-        kv_own(g, 'r').start()
-        kv_own(g, 'l').start()
-
-    def kv_in(c, g):
-        return remote(kv_ref.at[c, g], kv_ref.at[c, g], kvf_sem.at[g], kvr_sem.at[c, g], lane(right))
+    def kv_own(i, k):
+        ln, g = i % 2, i // 2
+        dev = (right * 2 + ln, left * 2 + ln, sib)[k]
+        return remote(ks_ref.at[ln, g], kv_ref.at[chip, g, own_rows], kvs_sem.at[k, i], kvr_sem.at[chip, g, core], {'sp': dev})
+
+    for i in range(n_k):
+        slot = w_wait(i, 'kv')
+        kv = product(xs_ref.at[:, own_rows], slot).astype(BF16)
+        ks_ref[i % 2, i // 2] = kv
+
+        @pl.when(core == i % 2)
+        def _():
+            kv_ref[chip, i // 2, own_rows] = kv
+        w_start(i + DEPTH, 'kv' if i + DEPTH < n_k else 'q')
+        if i == 0:
+            pl.semaphore_wait(barrier, group - 1)
+            x_copy.start()
+        kv_own(i, 0).start()
+        kv_own(i, 1).start()
+        pl.when(core != i % 2)(kv_own(i, 2).start)
+    tab_own.start()
+    for cp in tab_copies:
+        cp.start()
+
+    def kv_part(c, g, b, to):
+        ref = kv_ref.at[c, g, pl.ds(b * rows, rows)]
+        return remote(ref, ref, kvf_sem.at[g, b], kvr_sem.at[c, g, b], lane(to))
+
+    def kv_wait(c, g):
+        kv_part(c, g, 0, right).wait_recv()
+        kv_part(c, g, 1, right).wait_recv()
 
     def kv_relay(g):
-        kv_in(left, g).wait_recv()
-        kv_in(right, g).wait_recv()
-        if g < n_kv // 2:
-            remote(kv_ref.at[left, g], kv_ref.at[left, g], kvf_sem.at[g], kvr_sem.at[left, g], lane(right)).start()
-        else:
-            remote(kv_ref.at[right, g], kv_ref.at[right, g], kvf_sem.at[g], kvr_sem.at[right, g], lane(left)).start()
-
+        kv_wait(left, g)
+        kv_wait(right, g)
+        for b in range(2):
+            if g < n_kv // 2:
+                kv_part(left, g, b, right).start()
+            else:
+                kv_part(right, g, b, left).start()
+
+    x_copy.wait_recv()
+    x_copy.wait_send()
     def w_next(i):
         nxt = i + DEPTH
-        lap = (nxt - n_kv) // half
+        lap = (nxt - n_k) // half
 
         @pl.when((nxt < n_w) & (lax.rem(lap, 2) == 0))
         def _():
@@ -131,7 +146,7 @@
     def queries(r, lo, n):
         @pl.loop(lo, lo + n)
         def _(j):
-            i = n_kv + 2 * r * half + j
+            i = n_k + 2 * r * half + j
             slot = w_wait(i, 'q')
             q_ref[j] = product(xs_ref.at[:, r * rows:(r + 1) * rows], slot).astype(BF16)
             w_next(i)
@@ -207,7 +222,7 @@
     def project(r):
         @pl.loop(0, half)
         def _(j):
-            i = n_kv + (1 + 2 * r) * half + j
+            i = n_k + (1 + 2 * r) * half + j
             slot = w_wait(i, 'o')
             y = product(o_ref.at[r], slot)
             hs_ref[r, j] = (xs_ref[mine + j, r * rows:(r + 1) * rows].astype(F32) + y).astype(BF16)
@@ -255,6 +270,7 @@
         def _(g):
             if r == 0:
                 pl.when(g == 1)(lambda: kv_relay(n_kv - 1))
+                kv_part(chip, g, 1 - core, right).wait_recv()
             else:
                 pl.when((g == 1) & late)(lambda: relay(0, 0))
                 pl.when((g == 2) & last)(lambda: relay(1, 0))
@@ -271,7 +287,7 @@
         @pl.loop(0, n_kv)
         def _(g):
             if r == 0:
-                kv_in(opp, g).wait_recv()
+                kv_wait(opp, g)
 
             @pl.when(opp < chip)
             def _():
@@ -311,46 +327,63 @@
             def _():
                 h_relay(first, second, r, 0, j).wait_send()
                 h_relay(second, first, r, 1, j).wait_send()
+    for i in range(n_k):
+        kv_own(i, 0).wait_send()
+        kv_own(i, 1).wait_send()
+        pl.when(core != i % 2)(kv_own(i, 2).wait_send)
     for g in range(n_kv):
-        kv_own(g, 'r').wait_send()
-        kv_own(g, 'l').wait_send()
-        kv_in(left, g).wait_send()
-        for r in range(2):
-            o_copy(r, g).wait_send()
-    x_copy.wait_send()
+        for b in range(2):
+            kv_part(left, g, b, right).wait_send()
+            o_copy(b, g).wait_send()
     tab_own.wait()
     for cp in tab_copies:
         cp.wait()
 
 
-def route_kernel(tab_ref, h_ref, buf_ref, out_ref):
+def route_kernel(group, tab_ref, h_ref, buf_ref, out_ref, in_ref, st_ref, in_sem, st_sem, own_sem):
     me = lax.axis_index('sp')
-    s = pl.program_id(0)
-    rows = buf_ref.shape[0]
+    rows, width = out_ref.shape
     experts = tab_ref.shape[1] - 8
-    tab = tab_ref[0]
-    ids = tab[:2].astype(jnp.int32)
-    probs = tab[8:]
     exp_row = lax.broadcasted_iota(jnp.int32, (experts, rows), 0)
-    hit = jnp.max(jnp.where(ids == me, 1.0, 0.0), axis=0, keepdims=True)
-    both = jnp.where((exp_row == ids[0:1]) | (exp_row == ids[1:2]), probs, 0.0)
-    p_me = jnp.sum(jnp.where(exp_row == me, probs, 0.0), axis=0, keepdims=True)
-    gate = p_me * hit / jnp.sum(both, axis=0, keepdims=True)
     a = lax.broadcasted_iota(jnp.int32, (rows, rows), 0)
     b = lax.broadcasted_iota(jnp.int32, (rows, rows), 1)
     before = jnp.where(a < b, 1.0, 0.0).astype(BF16)
-    slot = jnp.dot(jnp.broadcast_to(hit, (8, rows)).astype(BF16), before, preferred_element_type=F32)[:1].astype(jnp.int32)
-    pick = (a == slot) & (hit > 0.5)
-    g_slot = jnp.sum(jnp.where(pick, gate, 0.0), axis=1, keepdims=True)
-    pick = jnp.where(pick, 1.0, 0.0).astype(BF16)
-    for j in range(buf_ref.shape[1] // CW):
-        cols = slice(j * CW, (j + 1) * CW)
-        got = jnp.dot(pick, h_ref[:, cols], preferred_element_type=F32)
-        buf_ref[:, cols] = (g_slot * got).astype(BF16)
-
-    @pl.when(s == me)
-    def _():
-        out_ref[...] = h_ref[...]
+
+    def fetch(s):
+        return pltpu.make_async_copy(h_ref.at[pl.ds(s * rows, rows)], in_ref.at[s], in_sem.at[s])
+
+    def put(s):
+        return pltpu.make_async_copy(st_ref.at[s % SLOTS], buf_ref.at[pl.ds(s * rows, rows)], st_sem.at[s])
+
+    own = pltpu.make_async_copy(in_ref.at[me], out_ref, own_sem)
+    for s in range(AHEAD):
+        fetch(s).start()
+    for s in range(group):
+        tab = tab_ref[s]
+        ids = tab[:2].astype(jnp.int32)
+        probs = tab[8:]
+        hit = jnp.max(jnp.where(ids == me, 1.0, 0.0), axis=0, keepdims=True)
+        both = jnp.where((exp_row == ids[0:1]) | (exp_row == ids[1:2]), probs, 0.0)
+        p_me = jnp.sum(jnp.where(exp_row == me, probs, 0.0), axis=0, keepdims=True)
+        gate = p_me * hit / jnp.sum(both, axis=0, keepdims=True)
+        slot = jnp.dot(jnp.broadcast_to(hit, (8, rows)).astype(BF16), before, preferred_element_type=F32)[:1].astype(jnp.int32)
+        pick = (a == slot) & (hit > 0.5)
+        g_slot = jnp.broadcast_to(jnp.sum(jnp.where(pick, gate, 0.0), axis=1, keepdims=True), (rows, CW))
+        pick = jnp.where(pick, 1.0, 0.0).astype(BF16)
+        fetch(s).wait()
+        if s + AHEAD < group:
+            fetch(s + AHEAD).start()
+        if s >= SLOTS:
+            put(s - SLOTS).wait()
+        for j in range(width // CW):
+            cols = slice(j * CW, (j + 1) * CW)
+            got = jnp.dot(pick, in_ref[s, :, cols], preferred_element_type=F32)
+            st_ref[s % SLOTS, :, cols] = (g_slot * got).astype(BF16)
+        put(s).start()
+    own.start()
+    for s in range(group - SLOTS, group):
+        put(s).wait()
+    own.wait()
 
 
 def solution(mesh):
@@ -383,6 +416,7 @@
                 pltpu.VMEM((n_col, crow, CW), BF16),
                 pltpu.VMEM((half, rows, CW), BF16),
                 pltpu.VMEM((2, n_col, rows, CW), BF16),
+                pltpu.VMEM((2, n_kv, rows, CW), BF16),
                 pltpu.VMEM((chips, n_kv, crow, CW), BF16),
                 pltpu.VMEM((DEPTH, width, CW), BF16),
                 pltpu.VMEM((2, half, rows, CW), BF16),
@@ -390,18 +424,23 @@
                 pltpu.VMEM((n_kv, 2, per * rows, HEAD), F32),
                 pltpu.VMEM((n_kv, 2, per * rows, HEAD), F32),
                 dma((DEPTH, 2)), dma((n_col,)), dma, dma,
-                dma((2, n_kv)), dma((chips, n_kv)), dma((n_kv,)), dma((2, n_kv)), dma((2, n_kv)),
+                dma((3, 2 * n_kv)), dma((chips, n_kv, 2)), dma((n_kv, 2)), dma((2, n_kv)), dma((2, n_kv)),
                 dma((4, 2, half)), dma((3, 2, half)), dma((2, 2, half)), dma((group, n_col)),
                 dma((group,)), dma((group,)),
             ],
             compiler_params=pltpu.CompilerParams(collective_id=0, has_side_effects=True, vmem_limit_bytes=56 * 1024 * 1024),
         )(x, w_q, w_k, w_v, w_o, tab)
         buf, hidden_out = pl.pallas_call(
-            route_kernel,
-            grid=(group,),
-            in_specs=[pl.BlockSpec((1, tab.shape[0], rows), lambda s: (s, 0, 0)), pl.BlockSpec((rows, width), lambda s: (s, 0))],
-            out_specs=[pl.BlockSpec((rows, width), lambda s: (s, 0)), pl.BlockSpec((rows, width), lambda s: (0, 0))],
+            functools.partial(route_kernel, group),
+            in_specs=[vm, hbm],
+            out_specs=[hbm, hbm],
             out_shape=[jax.ShapeDtypeStruct((group * rows, width), BF16), jax.ShapeDtypeStruct((rows, width), BF16)],
+            scratch_shapes=[
+                pltpu.VMEM((group, rows, width), BF16),
+                pltpu.VMEM((SLOTS, rows, width), BF16),
+                dma((group,)), dma((group,)), dma,
+            ],
+            compiler_params=pltpu.CompilerParams(vmem_limit_bytes=56 * 1024 * 1024),
         )(tabs, h_all)
         return hidden_out, buf[None]
 

time: 203 us -> 192 us (0.946)
  Pallas kernels: 199 us -> 188 us
    pallas_call x1, Pallas kernels: 176 us -> 170 us  [step(): pl.pallas_call(functools.partial(block_kernel, group), in_specs=[hbm] * 5...]
    pallas_call x1, Pallas kernels: 22.9 us -> 18.6 us  [step(): pl.pallas_call(functools.partial(route_kernel, group), in_specs=[vm, hbm]...]
where the time goes in v4:
time: 192 us; the launch traced here: 191 us
  Pallas kernels  188 us (98%)
  other arithmetic  2.06 us (1%)
    pallas_call x1, Pallas kernels, step(): pl.pallas_call(functools.partial(block_kernel, group), in_specs=[hbm] * 5...  170 us
    pallas_call x1, Pallas kernels, step(): pl.pallas_call(functools.partial(route_kernel, group), in_specs=[vm, hbm]...  18.6 us

profile of v4, /device:TPU:113, one launch (start us, length us, event | category | flops | bytes accessed | tf_op | source)
XLA Modules:
  0.0 191.3 jit_solution(9532575602334006388)
XLA Ops:
  0.6 0.1 pad.1.clone
  0.7 0.7 convert_bitcast_fusion
  1.4 1.4 pad_maximum_fusion.tab_ref
  2.8 169.7 %shard_map.86 = (bf16[2048,6144]{1,0:T(8,128)(2,1)}, f32[8,16,256]{2,1,0:T(8,128)}) custom-call(bf16[256,6144]{1,0:T(8,128)(2,1)} %x_ref.1, bf16[6144,6144]{1,0:T(8,128)(2,1)} %wq_ref.1, bf16[6144,1024]{1,0:T(8,128)(2,1)} %wk_ref.1, bf16[6144,1024]{1,0:T(8,128)(2,1)} %wv_ref.1, bf16[6144,6144]{1,0:T(8,128)(2,1)} %wo_ref.1, f32[16,256]{1,0:T(8,128)} %pad_maximum_fusion.tab_ref), custom_call_target="tpu_custom_call" | custom-call | tf_op jit(solution)/shard_map/pallas_call | solution.py:407
  172.5 18.6 %shard_map.87 = (bf16[2048,6144]{1,0:T(8,128)(2,1)}, bf16[256,6144]{1,0:T(8,128)(2,1)}) custom-call(f32[8,16,256]{2,1,0:T(8,128)} %get-tuple-element.6.tab_ref, bf16[2048,6144]{1,0:T(8,128)(2,1)} %get-tuple-element.7.h_ref), custom_call_target="tpu_custom_call" | custom-call | tf_op jit(solution)/shard_map/pallas_call | solution.py:433
  (1 shorter events, 0.0 us)

commit v5 on v4

--- a/solution.py
+++ b/solution.py
@@ -93,6 +93,21 @@
         dev = (right * 2 + ln, left * 2 + ln, sib)[k]
         return remote(ks_ref.at[ln, g], kv_ref.at[chip, g, own_rows], kvs_sem.at[k, i], kvr_sem.at[chip, g, core], {'sp': dev})
 
+    def to_right(c, low):
+        return (lax.rem(c + 1, chips) > c) | (low & (lax.rem(c + 2, chips) > c))
+
+    def to_left(c, low):
+        return (lax.rem(c + chips - 1, chips) > c) | (jnp.logical_not(low) & (lax.rem(c + 2, chips) > c))
+
+    def low_head(g):
+        return jnp.bool_(g < n_kv // 2)
+
+    def kv_sent(i, act):
+        low = low_head(i // 2)
+        pl.when(to_right(chip, low))(lambda: act(kv_own(i, 0)))
+        pl.when(to_left(chip, low))(lambda: act(kv_own(i, 1)))
+        pl.when(core != i % 2)(lambda: act(kv_own(i, 2)))
+
     for i in range(n_k):
         slot = w_wait(i, 'kv')
         kv = product(xs_ref.at[:, own_rows], slot).astype(BF16)
@@ -105,9 +120,7 @@
         if i == 0:
             pl.semaphore_wait(barrier, group - 1)
             x_copy.start()
-        kv_own(i, 0).start()
-        kv_own(i, 1).start()
-        pl.when(core != i % 2)(kv_own(i, 2).start)
+        kv_sent(i, lambda cp: cp.start())
     tab_own.start()
     for cp in tab_copies:
         cp.start()
@@ -120,14 +133,19 @@
         kv_part(c, g, 0, right).wait_recv()
         kv_part(c, g, 1, right).wait_recv()
 
+    def kv_passed(g, act):
+        c, to = (left, right) if g < n_kv // 2 else (right, left)
+
+        @pl.when(to > c)
+        def _():
+            for b in range(2):
+                act(kv_part(c, g, b, to))
+
     def kv_relay(g):
-        kv_wait(left, g)
-        kv_wait(right, g)
-        for b in range(2):
-            if g < n_kv // 2:
-                kv_part(left, g, b, right).start()
-            else:
-                kv_part(right, g, b, left).start()
+        low = low_head(g)
+        pl.when(to_right(left, low))(lambda: kv_wait(left, g))
+        pl.when(to_left(right, low))(lambda: kv_wait(right, g))
+        kv_passed(g, lambda cp: cp.start())
 
     x_copy.wait_recv()
     x_copy.wait_send()
@@ -272,8 +290,8 @@
                 pl.when(g == 1)(lambda: kv_relay(n_kv - 1))
                 kv_part(chip, g, 1 - core, right).wait_recv()
             else:
-                pl.when((g == 1) & late)(lambda: relay(0, 0))
-                pl.when((g == 2) & last)(lambda: relay(1, 0))
+                pl.when((g == 2) & late)(lambda: relay(0, 0))
+                pl.when((g == 3) & last)(lambda: relay(1, 0))
             blk(g, r, chip, (r + 1) * rows, True)
 
             @pl.loop(0, 2)
@@ -286,11 +304,10 @@
 
         @pl.loop(0, n_kv)
         def _(g):
-            if r == 0:
-                kv_wait(opp, g)
-
             @pl.when(opp < chip)
             def _():
+                if r == 0:
+                    kv_wait(opp, g)
                 blk(g, r, opp, 2 * rows, False)
             finish(g, r)
             o_copy(r, g).start()
@@ -328,12 +345,10 @@
                 h_relay(first, second, r, 0, j).wait_send()
                 h_relay(second, first, r, 1, j).wait_send()
     for i in range(n_k):
-        kv_own(i, 0).wait_send()
-        kv_own(i, 1).wait_send()
-        pl.when(core != i % 2)(kv_own(i, 2).wait_send)
+        kv_sent(i, lambda cp: cp.wait_send())
     for g in range(n_kv):
+        kv_passed(g, lambda cp: cp.wait_send())
         for b in range(2):
-            kv_part(left, g, b, right).wait_send()
             o_copy(b, g).wait_send()
     tab_own.wait()
     for cp in tab_copies:

time: 192 us -> 190 us (0.990)
  Pallas kernels: 188 us -> 186 us
    pallas_call x1, Pallas kernels: 170 us -> 168 us  [step(): pl.pallas_call(functools.partial(block_kernel, group), in_specs=[hbm] * 5...]
where the time goes in v5:
time: 190 us; the launch traced here: 189 us
  Pallas kernels  186 us (98%)
  other arithmetic  2.06 us (1%)
    pallas_call x1, Pallas kernels, step(): pl.pallas_call(functools.partial(block_kernel, group), in_specs=[hbm] * 5...  168 us
    pallas_call x1, Pallas kernels, step(): pl.pallas_call(functools.partial(route_kernel, group), in_specs=[vm, hbm]...  18.6 us

profile of v5, /device:TPU:113, one launch (start us, length us, event | category | flops | bytes accessed | tf_op | source)
XLA Modules:
  0.0 189.3 jit_solution(9282657877639163885)
XLA Ops:
  0.6 0.1 pad.1.clone
  0.7 0.7 convert_bitcast_fusion
  1.4 1.4 pad_maximum_fusion.tab_ref
  2.8 167.7 %shard_map.86 = (bf16[2048,6144]{1,0:T(8,128)(2,1)}, f32[8,16,256]{2,1,0:T(8,128)}) custom-call(bf16[256,6144]{1,0:T(8,128)(2,1)} %x_ref.1, bf16[6144,6144]{1,0:T(8,128)(2,1)} %wq_ref.1, bf16[6144,1024]{1,0:T(8,128)(2,1)} %wk_ref.1, bf16[6144,1024]{1,0:T(8,128)(2,1)} %wv_ref.1, bf16[6144,6144]{1,0:T(8,128)(2,1)} %wo_ref.1, f32[16,256]{1,0:T(8,128)} %pad_maximum_fusion.tab_ref), custom_call_target="tpu_custom_call" | custom-call | tf_op jit(solution)/shard_map/pallas_call | solution.py:422
  170.5 18.6 %shard_map.87 = (bf16[2048,6144]{1,0:T(8,128)(2,1)}, bf16[256,6144]{1,0:T(8,128)(2,1)}) custom-call(f32[8,16,256]{2,1,0:T(8,128)} %get-tuple-element.6.tab_ref, bf16[2048,6144]{1,0:T(8,128)(2,1)} %get-tuple-element.7.h_ref), custom_call_target="tpu_custom_call" | custom-call | tf_op jit(solution)/shard_map/pallas_call | solution.py:448
  (1 shorter events, 0.0 us)

commit v6 on v5

--- a/solution.py
+++ b/solution.py
@@ -71,8 +71,7 @@
     own_rows = pl.ds(pl.multiple_of(core * rows, rows), rows)
     for j in range(n_col):
         pltpu.make_async_copy(x_ref.at[:, pl.ds(j * CW, CW)], xs_ref.at[j, own_rows], x_sem.at[j]).start()
-    for i in range(DEPTH):
-        w_start(i, 'kv' if i < n_k else 'q')
+    w_start(0, 'kv')
 
     barrier = pltpu.get_barrier_semaphore()
     for d in range(1, group):
@@ -80,6 +79,8 @@
 
     for j in range(n_col):
         pltpu.make_async_copy(x_ref.at[:, pl.ds(j * CW, CW)], xs_ref.at[j, own_rows], x_sem.at[j]).wait()
+    for i in range(1, DEPTH):
+        w_start(i, 'kv' if i < n_k else 'q')
     x_copy = remote(xs_ref.at[:, own_rows], xs_ref.at[:, own_rows], xs_sem, xr_sem, {'sp': sib})
     tab_own = pltpu.make_async_copy(tab_ref, tabs_ref.at[me], ts_sem.at[0])
     tab_copies = [remote(tab_ref, tabs_ref.at[me], ts_sem.at[d], tr_sem.at[d], {'sp': lax.rem(me + d, group)}) for d in range(1, group)]

time: 190 us -> 187 us (0.984)
  Pallas kernels: 186 us -> 184 us
    pallas_call x1, Pallas kernels: 168 us -> 166 us  [step(): pl.pallas_call(functools.partial(block_kernel, group), in_specs=[hbm] * 5...]
where the time goes in v6:
time: 187 us
  Pallas kernels  184 us (98%)
  other arithmetic  2.06 us (1%)
    pallas_call x1, Pallas kernels, step(): pl.pallas_call(functools.partial(block_kernel, group), in_specs=[hbm] * 5...  166 us
    pallas_call x1, Pallas kernels, step(): pl.pallas_call(functools.partial(route_kernel, group), in_specs=[vm, hbm]...  18.6 us

profile of v6, /device:TPU:113, one launch (start us, length us, event | category | flops | bytes accessed | tf_op | source)
XLA Modules:
  0.0 187.1 jit_solution(16800472245801774251)
XLA Ops:
  0.6 0.1 pad.1.clone
  0.7 0.7 convert_bitcast_fusion
  1.4 1.4 pad_maximum_fusion.tab_ref
  2.8 165.5 %shard_map.86 = (bf16[2048,6144]{1,0:T(8,128)(2,1)}, f32[8,16,256]{2,1,0:T(8,128)}) custom-call(bf16[256,6144]{1,0:T(8,128)(2,1)} %x_ref.1, bf16[6144,6144]{1,0:T(8,128)(2,1)} %wq_ref.1, bf16[6144,1024]{1,0:T(8,128)(2,1)} %wk_ref.1, bf16[6144,1024]{1,0:T(8,128)(2,1)} %wv_ref.1, bf16[6144,6144]{1,0:T(8,128)(2,1)} %wo_ref.1, f32[16,256]{1,0:T(8,128)} %pad_maximum_fusion.tab_ref), custom_call_target="tpu_custom_call" | custom-call | tf_op jit(solution)/shard_map/pallas_call | solution.py:423
  168.3 18.6 %shard_map.87 = (bf16[2048,6144]{1,0:T(8,128)(2,1)}, bf16[256,6144]{1,0:T(8,128)(2,1)}) custom-call(f32[8,16,256]{2,1,0:T(8,128)} %get-tuple-element.6.tab_ref, bf16[2048,6144]{1,0:T(8,128)(2,1)} %get-tuple-element.7.h_ref), custom_call_target="tpu_custom_call" | custom-call | tf_op jit(solution)/shard_map/pallas_call | solution.py:449
  (1 shorter events, 0.0 us)
